TPU v7x, 32 devices: a whole 2x2x4 slice. The times are simulated.
32 devices in a mesh: row: 4 (over x, core), col: 8 (over z, y).
Axes of the slice: x: 2, y: 2, z: 4, core: 2. Of those that a mesh axis runs over, the one named last changes fastest.
Arguments:
- grid_tokens: bfloat16 [65536, 768], P(('row', 'col')), may hold values from -6 to 6
- grid_cotangent: bfloat16 [65536, 768], P(('row', 'col')), may hold values from -6 to 6
- send_rows: int32 [32, 512], P(('row', 'col')), may hold values from 0 to 2047, as said below
- send_counts: int32 [32, 32], P(('row', 'col')), may hold values from 1 to 16, as said below
- holder_segments: int32 [32, 512], P(('row', 'col')), may hold values from 0 to 3, as said below
- packed_master: float32 [768, 2304], P(('row', 'col')), may hold values from -0.21875 to 0.21875
- packed_first: float32 [768, 2304], P(('row', 'col')), may hold values from -80 to 80
- packed_second: float32 [768, 2304], P(('row', 'col')), may hold values from 430.8992 to 6897.664
- mixing_master: float32 [768, 768], P(('row', 'col')), may hold values from -1.75 to 1.75
- mixing_first: float32 [768, 768], P(('row', 'col')), may hold values from -12 to 12
- mixing_second: float32 [768, 768], P(('row', 'col')), may hold values from 9.66656 to 155.648
- expand_master: float32 [768, 3072], P(('row', 'col')), may hold values from -0.21875 to 0.21875
- expand_first: float32 [768, 3072], P(('row', 'col')), may hold values from -24 to 24
- expand_second: float32 [768, 3072], P(('row', 'col')), may hold values from 38.83008 to 620.9536
- reduce_master: float32 [3072, 768], P(('row', 'col')), may hold values from -0.109375 to 0.109375
- reduce_first: float32 [3072, 768], P(('row', 'col')), may hold values from -40 to 40
- reduce_second: float32 [3072, 768], P(('row', 'col')), may hold values from 107.80672 to 1720.32
- vector_master: float32 [12, 768], P(None, ('row', 'col')), may hold values from -1.2 to 1.3
- vector_first: float32 [12, 768], P(None, ('row', 'col')), may hold values from -128 to 128
- vector_second: float32 [12, 768], P(None, ('row', 'col')), may hold values from 969.9328 to 15515.648
Outputs:
- grid_output: bfloat16 [65536, 768], P(('row', 'col'))
- input_gradient: bfloat16 [65536, 768], P(('row', 'col'))
- packed_updated: float32 [768, 2304], P(('row', 'col'))
- packed_momentum: float32 [768, 2304], P(('row', 'col'))
- packed_variance: float32 [768, 2304], P(('row', 'col'))
- mixing_updated: float32 [768, 768], P(('row', 'col'))
- mixing_momentum: float32 [768, 768], P(('row', 'col'))
- mixing_variance: float32 [768, 768], P(('row', 'col'))
- expand_updated: float32 [768, 3072], P(('row', 'col'))
- expand_momentum: float32 [768, 3072], P(('row', 'col'))
- expand_variance: float32 [768, 3072], P(('row', 'col'))
- reduce_updated: float32 [3072, 768], P(('row', 'col'))
- reduce_momentum: float32 [3072, 768], P(('row', 'col'))
- reduce_variance: float32 [3072, 768], P(('row', 'col'))
- vector_updated: float32 [12, 768], P(None, ('row', 'col'))
- vector_momentum: float32 [12, 768], P(None, ('row', 'col'))
- vector_variance: float32 [12, 768], P(None, ('row', 'col'))
Inputs may be any that keep to these rules, and one draw needn't show every extreme that they name: `send_rows`: entries holder * 16 to holder * 16 + 15 of a source's row list grid rows of that source for that holder; the first send_counts of them are live, and all live rows of one source are distinct; the rest name arbitrary rows. `send_counts`: some holder gets 16 live rows from every source. `holder_segments`: slot s * 16 + j of a holder carries an item number below 3 if j < send_counts[s, holder], else 3.
All inputs are finite; a program needn't handle non-finite values.
Results may differ from a plain program's by a relative error of at most 0.012.
The roundings to bfloat16 on the way count: a program that leaves them out, or rounds other values in their place, can miss the bound.
Values may be sent and summed in bfloat16 or wider, within the bound.
No kernel may reach another device: no remote copies, remote signals or barrier semaphores. Data moves between devices by JAX's collectives and lax.ppermute only.
A program may use at most 192 MiB of HBM per device.

v0:
```python
import jax
import jax.numpy as jnp
from jax import lax
from jax.experimental import pallas as pl
from jax.experimental.pallas import tpu as pltpu
from jax.sharding import PartitionSpec as P

HEAD_DIM = 64


weight_rates = (0.07, 0.55, 0.07, 0.036, 0.4)
decay_rates = (0.05, 0.05, 0.05, 0.05, 0.0)


def normalize(values):
    center = values - jnp.mean(values, axis=-1, keepdims=True)
    spread = jnp.mean(center * center, axis=-1, keepdims=True)
    factor = lax.rsqrt(spread + 1e-06)
    return (center * factor, factor)


def norm_back(upstream, normed, factor, gain):
    scaled = upstream * gain
    return factor * (
        scaled
        - jnp.mean(scaled, axis=-1, keepdims=True)
        - normed * jnp.mean(scaled * normed, axis=-1, keepdims=True)
    )


def adamw(master, moment_one, moment_two, gradient, step_rate, decay_rate):
    first_new = 0.9 * moment_one + 0.1 * gradient
    second_new = 0.95 * moment_two + 0.05 * gradient * gradient
    moved = first_new / (1.0 - 0.9**10) / (jnp.sqrt(second_new / (1.0 - 0.95**10)) + 1e-08)
    return (master - step_rate * (moved + decay_rate * master), first_new, second_new)


AXES = ("row", "col")
HIDDEN_BLOCK = 768
TOKEN_BLOCK = 256
f32 = jnp.float32
bf16 = jnp.bfloat16


def dot(left, right, dims=((1,), (0,))):
    return lax.dot_general(left, right, (dims, ((), ())), preferred_element_type=f32)


def swap(values, bit):
    devices = lax.axis_size(AXES)
    return lax.ppermute(values, AXES, [(d, d ^ (1 << bit)) for d in range(devices)])


def bit_orders():
    rows, cols = lax.axis_size("row"), lax.axis_size("col")
    low_bits = cols.bit_length() - 1
    all_bits = (rows * cols).bit_length() - 1
    core, high, low = low_bits, list(range(low_bits + 1, all_bits)), list(range(low_bits))
    return ([core] + high + low, [core] + low[:1] + high + low[1:])


def place_of(order):
    count = len(order)
    return [
        sum(((r >> bit) & 1) << (count - 1 - step) for step, bit in enumerate(order))
        for r in range(1 << count)
    ]


def block_places(order):
    table = jnp.asarray(place_of(order), jnp.int32)
    ranks = jnp.arange(len(table), dtype=jnp.int32) ^ lax.axis_index(AXES)
    return jnp.take(table, ranks, mode="clip")


def by_place(blocks, order):
    table = place_of(order)
    back = [table.index(p) for p in range(len(table))]
    ranks = jnp.asarray(back, jnp.int32) ^ lax.axis_index(AXES)
    return jnp.take(blocks, ranks, axis=0, mode="clip")


class Chain:
    def __init__(self, keep, send, order, kind=bf16):
        self.keep, self.send, self.order, self.kind = keep, send, list(order), kind
        self.launch()

    def launch(self):
        self.got = swap(self.send, self.order.pop(0))

    def merge(self):
        half = self.keep.shape[0] // 2
        keep, got = self.keep, self.got
        self.send = (keep[half:].astype(f32) + got[half:].astype(f32)).astype(self.kind)
        self.keep = (keep[:half].astype(f32) + got[:half].astype(f32)).astype(self.kind)

    def total(self):
        return (self.keep.astype(f32) + self.got.astype(f32))[0]


def turn(values, chains):
    values, gots = lax.optimization_barrier((values, [c.got for c in chains]))
    for chain, got in zip(chains, gots):
        chain.got = got
        chain.merge()
    values, sends = lax.optimization_barrier((values, [c.send for c in chains]))
    for chain, part in zip(chains, sends):
        chain.send = part
        chain.launch()
    return values


def halves(blocks):
    half = blocks.shape[0] // 2
    return blocks[:half], blocks[half:]


def weight_chain(pairs, order):
    devices = lax.axis_size(AXES)
    keeps, sends = [], []
    for left, right in pairs:
        tokens, features = left.shape
        rows = features // devices
        turned = by_place(left.T.reshape(devices, rows, tokens), order)
        for side, parts in zip(halves(turned), (keeps, sends)):
            flat = dot(side.reshape(-1, tokens), right).astype(bf16)
            parts.append(flat.reshape(-1, rows, right.shape[1]))
    join = lambda parts: parts[0] if len(parts) == 1 else jnp.concatenate(parts, axis=-1)
    return Chain(join(keeps), join(sends), order)


class Gather:
    def __init__(self, shard, order):
        self.order, self.held, self.left = order, shard[None], list(reversed(order))
        self.launch()

    def launch(self):
        self.got = swap(self.held, self.left.pop(0))

    def merge(self):
        self.held = jnp.concatenate([self.held, self.got], axis=0)

    def blocks(self):
        self.merge()
        return jnp.take(self.held, block_places(self.order), axis=0, mode="clip")


def gather_turn(values, gathers):
    values, gots = lax.optimization_barrier((values, [g.got for g in gathers]))
    for gather, got in zip(gathers, gots):
        gather.got = got
        gather.merge()
    values, helds = lax.optimization_barrier((values, [g.held for g in gathers]))
    for gather, held in zip(gathers, helds):
        gather.held = held
        gather.launch()
    return values


def mlp_kernel(
    place_r, place_e, a2, dy, we, wr, bias,
    out_y, out_da, keep_r, send_r, keep_e, send_e, out_gb, u_all, dz_all, we_all,
):
    step = pl.program_id(0)
    tokens, features = a2.shape
    half = keep_r.shape[0]

    @pl.when(step == 0)
    def _():
        out_y[...] = jnp.zeros_like(out_y)
        out_da[...] = jnp.zeros_like(out_da)

    if len(we.shape) == 2:
        we_all[...] = we[...]
    else:
        rows_e = we.shape[1]
        for s in range(we.shape[0]):
            we_all[s * rows_e : (s + 1) * rows_e, :] = we[s]
    wr_all = wr[...].reshape(HIDDEN_BLOCK, features)

    def chunk(number, total):
        rows = pl.ds(pl.multiple_of(number * TOKEN_BLOCK, TOKEN_BLOCK), TOKEN_BLOCK)
        z = dot(a2[rows, :], we_all[...]) + bias[...]
        cumulative = 0.5 * (1.0 + lax.erf(z * 0.7071067811865476))
        u = (z * cumulative).astype(bf16)
        slope = cumulative + z * jnp.exp(-0.5 * z * z) * 0.3989422804014327
        dz = (dot(dy[rows, :], wr_all, ((1,), (1,))) * slope).astype(bf16)
        u_all[rows, :] = u
        dz_all[rows, :] = dz
        out_y[rows, :] += dot(u, wr_all)
        out_da[rows, :] += dot(dz, we_all[...], ((1,), (1,)))
        return total + jnp.sum(dz.astype(f32), axis=0, keepdims=True)

    out_gb[...] = lax.fori_loop(0, tokens // TOKEN_BLOCK, chunk, jnp.zeros(out_gb.shape, f32))

    def store(place, block, keep, send):
        @pl.when(place < half)
        def _():
            keep[place] = block

        @pl.when(place >= half)
        def _():
            send[place - half] = block

    rows_r = keep_r.shape[1]
    per_step = HIDDEN_BLOCK // rows_r
    grad = dot(u_all[...], dy[...], ((0,), (0,))).astype(bf16)
    for j in range(per_step):
        store(place_r[step * per_step + j], grad[j * rows_r : (j + 1) * rows_r], keep_r, send_r)
    grad = dot(a2[...], dz_all[...], ((0,), (0,))).astype(bf16)
    if len(keep_e.shape) == 2:
        keep_e[...] = grad
    else:
        rows_e = keep_e.shape[1]
        for s in range(2 * half):
            store(place_e[s], grad[s * rows_e : (s + 1) * rows_e], keep_e, send_e)


def mlp(a2, dy, both, bias, order_r, order_e):
    devices = lax.axis_size(AXES)
    tokens, features = a2.shape
    rows_r = both.shape[1] // 2
    hidden = devices * rows_r
    rows_e, wide = features // devices, hidden // features
    half = devices // 2
    direct = rows_e % 8 == 0
    whole = lambda *shape: pl.BlockSpec(shape, lambda i, *_: (0,) * len(shape))
    columns = pl.BlockSpec((features, HIDDEN_BLOCK), lambda i, *_: (0, i))
    if direct:
        we = both.reshape(devices, 2 * wide, rows_e, features)
        spec_we = pl.BlockSpec((devices, None, rows_e, features), lambda i, *_: (0, i, 0, 0))
        spec_e = [pl.BlockSpec((half, rows_e, HIDDEN_BLOCK), lambda i, *_: (0, 0, i))] * 2
        shape_e = [(half, rows_e, hidden)] * 2
    else:
        we = both[:, :rows_r].reshape(devices, wide, rows_e, features)
        we = we.transpose(0, 2, 1, 3).reshape(features, hidden)
        spec_we = columns
        spec_e = [columns, pl.BlockSpec((8, HIDDEN_BLOCK), lambda i, *_: (0, i))]
        shape_e = [(features, hidden), (8, hidden)]
    per_step = HIDDEN_BLOCK // rows_r
    grid_spec = pltpu.PrefetchScalarGridSpec(
        num_scalar_prefetch=2,
        grid=(hidden // HIDDEN_BLOCK,),
        in_specs=[
            whole(tokens, features),
            whole(tokens, features),
            spec_we,
            pl.BlockSpec((per_step, rows_r, features), lambda i, *_: (i, 1, 0)),
            pl.BlockSpec((1, HIDDEN_BLOCK), lambda i, *_: (0, i)),
        ],
        out_specs=[
            whole(tokens, features),
            whole(tokens, features),
            whole(half, rows_r, features),
            whole(half, rows_r, features),
            *spec_e,
            pl.BlockSpec((1, HIDDEN_BLOCK), lambda i, *_: (0, i)),
        ],
        scratch_shapes=[
            pltpu.VMEM((tokens, HIDDEN_BLOCK), bf16),
            pltpu.VMEM((tokens, HIDDEN_BLOCK), bf16),
            pltpu.VMEM((features, HIDDEN_BLOCK), bf16),
        ],
    )
    y, da2, keep_r, send_r, keep_e, send_e, grad_b = pl.pallas_call(
        mlp_kernel,
        grid_spec=grid_spec,
        out_shape=[
            jax.ShapeDtypeStruct((tokens, features), f32),
            jax.ShapeDtypeStruct((tokens, features), f32),
            jax.ShapeDtypeStruct((half, rows_r, features), bf16),
            jax.ShapeDtypeStruct((half, rows_r, features), bf16),
            jax.ShapeDtypeStruct(shape_e[0], bf16),
            jax.ShapeDtypeStruct(shape_e[1], bf16),
            jax.ShapeDtypeStruct((1, hidden), f32),
        ],
        compiler_params=pltpu.CompilerParams(
            dimension_semantics=("arbitrary",), vmem_limit_bytes=56 << 20
        ),
        cost_estimate=pl.CostEstimate(
            flops=12 * tokens * features * hidden,
            transcendentals=2 * tokens * hidden,
            bytes_accessed=8 * features * hidden + 12 * tokens * features,
        ),
        name="mlp",
    )(block_places(order_r), block_places(order_e), a2, dy, we, both, bias[None])
    if not direct:
        keep_e, send_e = halves(by_place(keep_e.reshape(devices, rows_e, hidden), order_e))
    return y, da2, (keep_r, send_r), (keep_e, send_e), grad_b


def head_lanes(shape, head):
    lane = lax.broadcasted_iota(jnp.int32, shape, 1)
    return (lane >= head * HEAD_DIM) & (lane < (head + 1) * HEAD_DIM)


def scaled_scores(q, k, seg_col, seg_row):
    scores = dot(q, k, ((1,), (1,))) * HEAD_DIM ** (-0.5)
    return jnp.where(seg_col == seg_row, scores, -1e30)


def attend_kernel(q, k, v, seg_col, seg_row, out, out_lse):
    both_out, both_lse = [], []
    for head in range(2):
        mine = head_lanes(q.shape, head)
        q_head = jnp.where(mine, q[...].astype(f32), 0.0).astype(bf16)
        scores = scaled_scores(q_head, k[...], seg_col[...], seg_row[...])
        highest = jnp.max(scores, axis=-1, keepdims=True)
        weights = jnp.exp(scores - highest)
        total = jnp.sum(weights, axis=-1, keepdims=True)
        shares = (weights / total).astype(bf16)
        both_out.append(dot(shares, v[...]))
        both_lse.append(highest + jnp.log(total))
    first = head_lanes(q.shape, 0)
    out[...] = jnp.where(first, both_out[0], both_out[1]).astype(bf16)
    out_lse[...] = jnp.where(first, both_lse[0], both_lse[1])


def attend_back_kernel(q, k, v, d_out, lse, seg_col, seg_row, out_dq, out_dk, out_dv):
    parts = []
    for head in range(2):
        mine = head_lanes(q.shape, head)
        q_head = jnp.where(mine, q[...].astype(f32), 0.0).astype(bf16)
        d_head = jnp.where(mine, d_out[...].astype(f32), 0.0).astype(bf16)
        scores = scaled_scores(q_head, k[...], seg_col[...], seg_row[...])
        chances = jnp.exp(scores - lse[:, head * HEAD_DIM : head * HEAD_DIM + 1])
        d_chances = dot(d_head, v[...], ((1,), (1,)))
        row_dot = jnp.sum(chances * d_chances, axis=-1, keepdims=True)
        d_scores = (chances * (d_chances - row_dot)).astype(bf16)
        parts.append(
            (
                dot(d_scores, k[...]) * HEAD_DIM ** (-0.5),
                dot(d_scores, q[...], ((0,), (0,))) * HEAD_DIM ** (-0.5),
                dot(chances.astype(bf16), d_out[...], ((0,), (0,))),
            )
        )
    first = head_lanes(q.shape, 0)
    for ref, left, right in zip((out_dq, out_dk, out_dv), *parts):
        ref[...] = jnp.where(first, left, right).astype(bf16)


def attention(query_key, values, segments, extra=None):
    tokens, features = values.shape
    pairs = features // (2 * HEAD_DIM)
    head = pl.BlockSpec((tokens, 2 * HEAD_DIM), lambda i: (0, i))
    key = pl.BlockSpec((tokens, 2 * HEAD_DIM), lambda i: (0, i + pairs))
    whole = lambda *shape: pl.BlockSpec(shape, lambda i: (0,) * len(shape))
    segs = [segments[:, None], segments[None, :]]
    seg_specs = [whole(tokens, 1), whole(1, tokens)]
    shape = lambda kind: jax.ShapeDtypeStruct((tokens, features), kind)
    more = [] if extra is None else list(extra)
    outs = [shape(bf16), shape(f32)] if extra is None else [shape(bf16)] * 3
    products = 2 if extra is None else 5
    return pl.pallas_call(
        attend_kernel if extra is None else attend_back_kernel,
        grid=(pairs,),
        in_specs=[head, key, head] + [head] * len(more) + seg_specs,
        out_specs=[head] * len(outs),
        out_shape=outs,
        compiler_params=pltpu.CompilerParams(
            dimension_semantics=("arbitrary",), vmem_limit_bytes=48 << 20
        ),
        cost_estimate=pl.CostEstimate(
            flops=4 * products * tokens * tokens * features,
            transcendentals=2 * pairs * tokens * tokens,
            bytes_accessed=16 * tokens * features,
        ),
        name="attend" if extra is None else "attend_back",
    )(query_key, query_key, values, *more, *segs)


def on_device(
    grid_tokens,
    grid_cotangent,
    send_rows,
    send_counts,
    holder_segments,
    packed_master,
    packed_first,
    packed_second,
    mixing_master,
    mixing_first,
    mixing_second,
    expand_master,
    expand_first,
    expand_second,
    reduce_master,
    reduce_first,
    reduce_second,
    vector_master,
    vector_first,
    vector_second,
):
    devices = lax.axis_size(AXES)
    holding = send_rows.shape[1]
    slot_rows = holding // devices
    tokens, features = grid_tokens.shape
    first, second = bit_orders()
    segments = holder_segments[0]

    slots = jnp.arange(slot_rows, dtype=jnp.int32)[None, :]
    live = (slots < send_counts[0][:, None]).reshape(holding)
    row_index = jnp.where(live, send_rows[0], -1)
    pick = (row_index[:, None] == jnp.arange(tokens, dtype=jnp.int32)[None, :]).astype(bf16)

    def send(rows):
        blocks = rows.reshape(devices, slot_rows, features)
        moved = lax.all_to_all(blocks, AXES, split_axis=0, concat_axis=0, tiled=True)
        return moved.reshape(holding, features)

    def put_rows(rows):
        return dot(pick, rows, ((0,), (0,))).astype(bf16)

    low = packed_master.astype(bf16)
    cut = 2 * features
    lines = vector_master.shape[0]
    padded = jnp.pad(vector_master.T.astype(bf16), ((0, 0), (0, 128 - lines)))
    late = jnp.concatenate([low[:, cut:], mixing_master.astype(bf16), padded], axis=1)
    gathers = [Gather(low[:, :cut], first), Gather(late, second)]
    rows_e, hidden = expand_master.shape
    tall = expand_master.astype(bf16).reshape(rows_e, hidden // features, features)
    tall = tall.transpose(1, 0, 2).reshape(-1, features)
    tall = jnp.concatenate([tall, reduce_master.astype(bf16)], axis=0)
    w_mlp = lax.all_gather(tall, AXES, axis=0, tiled=False)

    picked = dot(pick, grid_tokens).astype(bf16)
    picked_grad = dot(pick, grid_cotangent).astype(bf16)
    low_stages = lax.axis_size("col").bit_length() - 2
    while gathers[0].left:
        stage = len(first) - len(gathers[0].left)
        if stage == low_stages:
            picked = gather_turn(picked, gathers)
            arrived = send(picked)
        elif len(gathers[0].left) == 1:
            picked_grad = gather_turn(picked_grad, gathers)
            arrived_grad = send(picked_grad)
        else:
            gather_turn((), gathers)
    early = gathers[0].blocks().reshape(features, cut)
    late = gathers[1].blocks().reshape(features, 2 * features + 128)
    w_value, w_mixing = late[:, :features], late[:, features : 2 * features]
    vectors = late[:, 2 * features : 2 * features + lines].T.astype(f32)
    gain_one, shift_one, bias_query, bias_value, bias_mixing = (vectors[i] for i in range(5))
    gain_two, shift_two, bias_output = (vectors[i] for i in range(5, 8))
    bias_hidden = vectors[8:].reshape(-1)

    inputs = arrived.astype(f32)
    normed_one, factor_one = normalize(inputs)
    layer_one = (normed_one * gain_one + shift_one).astype(bf16)
    joined_bias = jnp.concatenate([bias_query, jnp.zeros_like(bias_query)])
    query_key = (dot(layer_one, early) + joined_bias).astype(bf16)
    values = (dot(layer_one, w_value) + bias_value).astype(bf16)
    attended, log_total = attention(query_key, values, segments)
    middle = inputs + dot(attended, w_mixing) + bias_mixing
    normed_two, factor_two = normalize(middle)
    layer_two = (normed_two * gain_two + shift_two).astype(bf16)
    branch, d_layer_two, grad_reduce, grad_expand, grad_hidden = mlp(
        layer_two, arrived_grad, w_mlp, bias_hidden, first, second
    )
    chain_reduce = Chain(*grad_reduce, first)
    chain_expand = Chain(*grad_expand, second)
    chains = [chain_reduce, chain_expand]
    outputs = (middle + branch + bias_output).astype(bf16)

    upstream = arrived_grad.astype(f32)
    d_middle = upstream + norm_back(d_layer_two, normed_two, factor_two, gain_two)
    d_branch = d_middle.astype(bf16)
    d_attended = dot(d_branch, w_mixing, ((1,), (1,))).astype(bf16)
    early_reads = (d_attended, outputs, layer_one, attended, d_branch, d_layer_two, normed_two, upstream)
    early_reads = turn(early_reads, chains)
    d_attended, outputs, layer_one, attended, d_branch, d_layer_two, normed_two, upstream = early_reads
    moved = send(outputs)
    d_query, d_key, d_value = attention(query_key, values, segments, (d_attended, log_total))
    chain_late = weight_chain([(layer_one, d_value), (attended, d_branch)], first)
    chain_query_key = weight_chain([(layer_one, d_query), (layer_one, d_key)], second)
    chains += [chain_late, chain_query_key]
    d_query_key = jnp.concatenate([d_query, d_key], axis=1)
    d_layer_one = dot(d_query_key, early, ((1,), (1,))) + dot(d_value, w_value, ((1,), (1,)))
    input_grads = d_middle + norm_back(d_layer_one, normed_one, factor_one, gain_one)
    input_grads = input_grads.astype(bf16)
    total = lambda part: jnp.sum(part.astype(f32), axis=0, keepdims=True)
    grad_vector = jnp.concatenate(
        [
            total(d_layer_one * normed_one),
            total(d_layer_one),
            total(d_query),
            total(d_value),
            total(d_branch),
            total(d_layer_two * normed_two),
            total(d_layer_two),
            total(upstream),
            grad_hidden.reshape(-1, features),
        ],
        axis=0,
    )
    vector_blocks = grad_vector.T.reshape(devices, -1, lines)
    vector_blocks = by_place(vector_blocks, second)
    input_grads, vector_blocks, moved = turn((input_grads, vector_blocks, moved), chains)
    moved_grad = send(input_grads)
    chain_vector = Chain(*halves(vector_blocks), second, f32)
    chains.append(chain_vector)
    moved = turn(moved, chains)
    grid_output = put_rows(moved)
    moved_grad = turn(moved_grad, chains)
    input_gradient = put_rows(moved_grad)
    while any(chain.order for chain in chains):
        turn((), [chain for chain in chains if chain.order])
    masters = (packed_master, mixing_master, expand_master, reduce_master, vector_master)
    firsts = (packed_first, mixing_first, expand_first, reduce_first, vector_first)
    seconds = (packed_second, mixing_second, expand_second, reduce_second, vector_second)
    late_sum = chain_late.total()
    shares = (
        jnp.concatenate([chain_query_key.total(), late_sum[:, :features]], axis=1),
        late_sum[:, features:],
        chain_expand.total(),
        chain_reduce.total(),
        chain_vector.total().T,
    )
    updates = [
        adamw(
            masters[number],
            firsts[number],
            seconds[number],
            shares[number],
            weight_rates[number],
            decay_rates[number],
        )
        for number in range(5)
    ]
    return (
        grid_output,
        input_gradient,
        updates[0][0],
        updates[0][1],
        updates[0][2],
        updates[1][0],
        updates[1][1],
        updates[1][2],
        updates[2][0],
        updates[2][1],
        updates[2][2],
        updates[3][0],
        updates[3][1],
        updates[3][2],
        updates[4][0],
        updates[4][1],
        updates[4][2],
    )


def solution(mesh):
    in_specs = (
        P(("row", "col"), None),
        P(("row", "col"), None),
        P(("row", "col"), None),
        P(("row", "col"), None),
        P(("row", "col"), None),
        P(("row", "col"), None),
        P(("row", "col"), None),
        P(("row", "col"), None),
        P(("row", "col"), None),
        P(("row", "col"), None),
        P(("row", "col"), None),
        P(("row", "col"), None),
        P(("row", "col"), None),
        P(("row", "col"), None),
        P(("row", "col"), None),
        P(("row", "col"), None),
        P(("row", "col"), None),
        P(None, ("row", "col")),
        P(None, ("row", "col")),
        P(None, ("row", "col")),
    )
    out_specs = (
        P(("row", "col"), None),
        P(("row", "col"), None),
        P(("row", "col"), None),
        P(("row", "col"), None),
        P(("row", "col"), None),
        P(("row", "col"), None),
        P(("row", "col"), None),
        P(("row", "col"), None),
        P(("row", "col"), None),
        P(("row", "col"), None),
        P(("row", "col"), None),
        P(("row", "col"), None),
        P(("row", "col"), None),
        P(("row", "col"), None),
        P(None, ("row", "col")),
        P(None, ("row", "col")),
        P(None, ("row", "col")),
    )
    return jax.shard_map(
        on_device, mesh=mesh, in_specs=in_specs, out_specs=out_specs, check_vma=False
    )
```

profile of v0, /device:TPU:30, one launch (start us, length us, event | category | flops | bytes accessed | tf_op | source)
XLA Modules:
  0.0 353.8 jit_solution(8342473933573802372)
XLA Ops:
  11.5 2.7 collective-permute-start.1
  15.0 3.6 %collective-permute-done = bf16[1,24,1536]{2,1,0:T(8,128)(2,1)S(1)} collective-permute-done((bf16[1,24,1536]{2,1,0:T(8,128)(2,1)S(1)}, bf16[1,24,1536]{2,1,0:T(8,128)(2,1)S(1)}, u32[]{:S(2)}, u32[]{:S(2)}) %collective-permute-start) | collective-permute-done | bytes 73760 | tf_op jit(solution)/shard_map/ppermute | solution.py:51
  18.5 1.6 collective-permute-done.1
  20.2 2.0 collective-permute-start.3
  22.2 2.8 fusion.39
  25.1 4.8 %collective-permute-done.2 = bf16[2,24,1536]{2,1,0:T(8,128)(2,1)S(1)} collective-permute-done((bf16[2,24,1536]{2,1,0:T(8,128)(2,1)S(1)}, bf16[2,24,1536]{2,1,0:T(8,128)(2,1)S(1)}, u32[]{:S(2)}, u32[]{:S(2)}) %collective-permute-start.2) | collective-permute-done | bytes 147488 | tf_op jit(solution)/shard_map/ppermute | solution.py:51
  29.9 5.8 %collective-permute-done.3 = bf16[2,24,1664]{2,1,0:T(8,128)(2,1)S(1)} collective-permute-done((bf16[2,24,1664]{2,1,0:T(8,128)(2,1)S(1)}, bf16[2,24,1664]{2,1,0:T(8,128)(2,1)S(1)}, u32[]{:S(2)}, u32[]{:S(2)}) %collective-permute-start.3) | collective-permute-done | bytes 159776 | tf_op jit(solution)/shard_map/ppermute | solution.py:51
  36.9 10.7 %collective-permute-done.4 = bf16[4,24,1536]{2,1,0:T(8,128)(2,1)S(1)} collective-permute-done((bf16[4,24,1536]{2,1,0:T(8,128)(2,1)S(1)}, bf16[4,24,1536]{2,1,0:T(8,128)(2,1)S(1)}, u32[]{:S(2)}, u32[]{:S(2)}) %collective-permute-start.4) | collective-permute-done | bytes 294944 | tf_op jit(solution)/shard_map/ppermute | solution.py:51
  48.5 2.2 collective-permute-start.6
  50.7 6.3 %all-to-all-start.1 = ((bf16[32,16,768]{2,1,0:T(8,128)(2,1)}), bf16[32,16,768]{2,1,0:T(8,128)(2,1)S(1)}, u32[]{:S(2)}, u32[]{:S(2)}) async-start(bf16[32,16,768]{2,1,0:T(8,128)(2,1)} %bitcast.7), calls=%async_computation.1 | async-start | bytes 1572864 | tf_op jit(solution)/shard_map/all_to_all | solution.py:408
  57.1 4.7 %fusion.38 = bf16[512,768]{1,0:T(8,128)(2,1)} fusion(bf16[2048,768]{1,0:T(8,128)(2,1)} %param.30, s32[512]{0:T(512)S(1)} %broadcast_select_fusion), kind=kOutput, calls=%fused_computation.68 | convolution fusion | flops 1612054528 | bytes 3934208 | tf_op jit(solution)/shard_map/dot_general | solution.py:46
  61.8 9.9 %collective-permute-done.6 = bf16[8,24,1536]{2,1,0:T(8,128)(2,1)S(1)} collective-permute-done((bf16[8,24,1536]{2,1,0:T(8,128)(2,1)S(1)}, bf16[8,24,1536]{2,1,0:T(8,128)(2,1)S(1)}, u32[]{:S(2)}, u32[]{:S(2)}) %collective-permute-start.6) | collective-permute-done | bytes 589856 | tf_op jit(solution)/shard_map/ppermute | solution.py:51
  75.2 4.0 %all-to-all-done.1 = bf16[32,16,768]{2,1,0:T(8,128)(2,1)S(1)} async-done(((bf16[32,16,768]{2,1,0:T(8,128)(2,1)}), bf16[32,16,768]{2,1,0:T(8,128)(2,1)S(1)}, u32[]{:S(2)}, u32[]{:S(2)}) %all-to-all-start.1) | async-done | bytes 786464 | tf_op jit(solution)/shard_map/all_to_all | solution.py:408
  79.2 7.6 %all-to-all-start = ((bf16[32,16,768]{2,1,0:T(8,128)(2,1)}), bf16[32,16,768]{2,1,0:T(8,128)(2,1)}, u32[]{:S(2)}, u32[]{:S(2)}) async-start(bf16[32,16,768]{2,1,0:T(8,128)(2,1)} %bitcast.175), calls=%async_computation | async-start | bytes 1572864 | tf_op jit(solution)/shard_map/all_to_all | solution.py:408
  87.6 3.2 pad_maximum_fusion.1
  90.9 3.8 %gather_fusion.3 = bf16[32,24,1536]{2,1,0:T(8,128)(2,1)} fusion(bf16[32,24,1536]{2,1,0:T(8,128)(2,1)} %pad_maximum_fusion.1, s32[1024]{0:T(1024)S(1)} %pad_clamp_fusion.2), kind=kCustom, calls=%fused_computation.3 | custom fusion | bytes 4718720 | tf_op jit(solution)/shard_map/jit(_take)/gather | solution.py:145
  94.7 3.0 pad_maximum_fusion
  97.7 4.0 %gather_fusion.1 = bf16[32,24,1664]{2,1,0:T(8,128)(2,1)} fusion(bf16[32,24,1664]{2,1,0:T(8,128)(2,1)} %pad_maximum_fusion, s32[1024]{0:T(1024)S(1)} %pad_clamp_fusion.3), kind=kCustom, calls=%fused_computation.1 | custom fusion | bytes 5111936 | tf_op jit(solution)/shard_map/jit(_take)/gather | solution.py:145
  106.6 1.4 fusion.6.q.k
  108.8 9.2 %attend.1 = (bf16[512,768]{1,0:T(8,128)(2,1)S(1)}, f32[512,768]{1,0:T(8,128)S(1)}) custom-call(bf16[512,1536]{1,0:T(8,128)(2,1)S(1)} %fusion.6.q.k, bf16[512,1536]{1,0:T(8,128)(2,1)S(1)} %fusion.6.q.k, bf16[512,768]{1,0:T(8,128)(2,1)S(1)} %add_convert_fusion.6.v, s32[512,1]{1,0:T(8,128)S(1)} %copy.51.seg_col, s32[1,512]{1,0:T(1,128)S(1)} %copy-done.2), custom_call_target="tpu_custom_call" | custom-call | flops 1610612736 | bytes 6291456 | tf_op jit(solution)/shard_map/attend/pallas_call | solution.py:354
  121.4 3.2 all-gather.3.cloned.1.call-done
  124.7 30.4 %mlp.1 = (f32[512,768]{1,0:T(8,128)}, f32[512,768]{1,0:T(8,128)}, bf16[16,96,768]{2,1,0:T(8,128)(2,1)}, bf16[16,96,768]{2,1,0:T(8,128)(2,1)}, bf16[16,24,3072]{2...) custom-call(s32[32]{0:T(128)} %copy-done.81, s32[32]{0:T(128)} %copy-done.80, ...), custom_call_target="tpu_custom_call" | custom-call | flops 14495514624 | bytes 23592960 | tf_op jit(solution)/shard_map/mlp/pallas_call | solution.py:265
  156.3 2.5 bitcast_convert_fusion
  160.0 3.9 %multiply_reduce_fusion.4 = (f32[512]{0:T(512)S(1)}, f32[512]{0:T(512)S(1)}, bf16[512,768]{1,0:T(8,128)(2,1)}) fusion(f32[512,768]{1,0:T(8,128)} %get-tuple-element.156, f32[768]{0:T(1024)S(1)} %get-tuple-element.219, f32[512,768]{1,0:T(8,128)S(1)} %get-tuple-element.157, f32[768]{0:T(1024)S(1)} %get-tuple-element.217, f32[512,768]{1,0:T(8,128)} %copy-done.15, ...), kind=kLoop, calls=%fused_computation.71 | loop fusion | flops 2751488 | bytes 7088128 | tf_op jit(solution)/shard_map/reduce_sum | solution.py:26
  163.9 2.7 fusion.69
  168.8 3.9 %add_convert_fusion.1 = (bf16[8,96,768]{2,1,0:T(8,128)(2,1)}, bf16[8,96,768]{2,1,0:T(8,128)(2,1)}) fusion(bf16[16,96,768]{2,1,0:T(8,128)(2,1)} %collective-permute-done.10, bf16[16,96,768]{2,1,0:T(8,128)(2,1)S(1)} %copy-done.29), kind=kLoop, calls=%fused_computation.20 | loop fusion | flops 4718592 | bytes 7077888 | tf_op jit(solution)/shard_map/convert_element_type | solution.py:95
  172.6 4.1 %add_convert_fusion = (bf16[8,24,3072]{2,1,0:T(8,128)(2,1)}, bf16[8,24,3072]{2,1,0:T(8,128)(2,1)}) fusion(bf16[16,24,3072]{2,1,0:T(8,128)(2,1)} %collective-permute-done.11, bf16[16,24,3072]{2,1,0:T(8,128)(2,1)S(1)} %copy-done.28), kind=kLoop, calls=%fused_computation.19 | loop fusion | flops 4718592 | bytes 7077888 | tf_op jit(solution)/shard_map/convert_element_type | solution.py:95
  176.7 15.0 %attend_back.1 = (bf16[512,768]{1,0:T(8,128)(2,1)S(1)}, bf16[512,768]{1,0:T(8,128)(2,1)S(1)}, bf16[512,768]{1,0:T(8,128)(2,1)S(1)}) custom-call(bf16[512,1536]{1,0:T(8,128)(2,1)S(1)} %copy-done.4, bf16[512,1536]{1,0:T(8,128)(2,1)S(1)} %copy-done.4, bf16[512,768]{1,0:T(8,128)(2,1)S(1)} %copy-done.7, bf16[512,768]{1,0:T(8,128)(2,1)S(1)} %convolution_convert_fusion.d_out, ...), custom_call_target="tpu_custom_call" | custom-call | flops 4026531840 | bytes 6291456 | tf_op jit(solution)/shard_map/attend_back/pallas_call | solution.py:354
  191.7 2.0 fusion.42
  195.2 2.3 copy.55
  197.5 2.6 gather_fusion.7
  200.1 1.3 fusion.70
  201.4 1.3 convolution_convert_fusion.6
  202.8 1.3 convolution_convert_fusion.5
  204.1 3.4 fusion.33
  208.1 6.2 %all-to-all-start.2 = ((bf16[32,16,768]{2,1,0:T(8,128)(2,1)}), bf16[32,16,768]{2,1,0:T(8,128)(2,1)}, u32[]{:S(2)}, u32[]{:S(2)}) async-start(bf16[32,16,768]{2,1,0:T(8,128)(2,1)} %bitcast.155), calls=%async_computation.2 | async-start | bytes 1572864 | tf_op jit(solution)/shard_map/all_to_all | solution.py:408
  216.6 2.8 gather_fusion.5
  219.4 1.6 gather_fusion.6
  221.0 2.0 fusion.71
  230.5 1.5 reduce_sum.159
  232.4 1.4 gather_fusion.4
  233.8 1.3 convolution_convert_fusion.2
  235.1 2.5 convolution_convert_fusion.3
  237.6 1.3 convolution_convert_fusion.4
  239.0 1.4 fusion.32
  240.4 9.3 %collective-permute-done.12 = bf16[8,96,768]{2,1,0:T(8,128)(2,1)} collective-permute-done((bf16[8,96,768]{2,1,0:T(8,128)(2,1)}, bf16[8,96,768]{2,1,0:T(8,128)(2,1)}, u32[]{:S(2)}, u32[]{:S(2)}) %collective-permute-start.12) | collective-permute-done | bytes 1179680 | tf_op jit(solution)/shard_map/ppermute | solution.py:51
  249.7 2.5 add_convert_fusion.10
  252.2 2.6 add_convert_fusion.9
  254.8 2.4 add_convert_fusion.8
  257.2 2.4 add_convert_fusion.7
  261.5 1.4 collective-permute-start.18
  263.8 6.4 %all-to-all-start.3 = ((bf16[32,16,768]{2,1,0:T(8,128)(2,1)}), bf16[32,16,768]{2,1,0:T(8,128)(2,1)}, u32[]{:S(2)}, u32[]{:S(2)}) async-start(bf16[32,16,768]{2,1,0:T(8,128)(2,1)} %bitcast.40), calls=%async_computation.3 | async-start | bytes 1572864 | tf_op jit(solution)/shard_map/all_to_all | solution.py:408
  270.2 9.9 %collective-permute-done.16 = bf16[4,96,768]{2,1,0:T(8,128)(2,1)} collective-permute-done((bf16[4,96,768]{2,1,0:T(8,128)(2,1)}, bf16[4,96,768]{2,1,0:T(8,128)(2,1)}, u32[]{:S(2)}, u32[]{:S(2)}) %collective-permute-start.16) | collective-permute-done | bytes 589856 | tf_op jit(solution)/shard_map/ppermute | solution.py:51
  280.1 1.9 collective-permute-done.17
  282.0 14.2 %collective-permute-done.18 = bf16[8,24,1536]{2,1,0:T(8,128)(2,1)} collective-permute-done((bf16[8,24,1536]{2,1,0:T(8,128)(2,1)}, bf16[8,24,1536]{2,1,0:T(8,128)(2,1)}, u32[]{:S(2)}, u32[]{:S(2)}) %collective-permute-start.18) | collective-permute-done | bytes 589856 | tf_op jit(solution)/shard_map/ppermute | solution.py:51
  302.7 1.4 collective-permute-start.24
  304.5 4.7 %fusion.4 = bf16[2048,768]{1,0:T(8,128)(2,1)} fusion(bf16[512,768]{1,0:T(8,128)(2,1)} %bitcast.21, s32[512]{0:T(512)S(1)} %copy-done.78), kind=kOutput, calls=%fused_computation.13 | convolution fusion | flops 1613234176 | bytes 3934208 | tf_op jit(solution)/shard_map/dot_general | solution.py:46
  310.0 3.2 collective-permute-done.22
  316.0 4.7 %fusion.5 = bf16[2048,768]{1,0:T(8,128)(2,1)} fusion(bf16[512,768]{1,0:T(8,128)(2,1)} %bitcast.41, s32[512]{0:T(512)S(1)} %copy-done.78), kind=kOutput, calls=%fused_computation.14 | convolution fusion | flops 1613234176 | bytes 3934208 | tf_op jit(solution)/shard_map/dot_general | solution.py:46
  321.6 2.2 collective-permute-start.32
  324.7 2.2 collective-permute-start.29
  327.7 5.8 %collective-permute-done.31 = bf16[1,24,3072]{2,1,0:T(8,128)(2,1)S(1)} collective-permute-done((bf16[1,24,3072]{2,1,0:T(8,128)(2,1)S(1)}, bf16[1,24,3072]{2,1,0:T(8,128)(2,1)S(1)}, u32[]{:S(2)}, u32[]{:S(2)}) %collective-permute-start.31) | collective-permute-done | bytes 147488 | tf_op jit(solution)/shard_map/ppermute | solution.py:51
  334.6 5.1 %collective-permute-done.33 = f32[2,24,12]{1,2,0:T(8,128)S(1)} collective-permute-done((f32[2,24,12]{1,2,0:T(8,128)S(1)}, f32[2,24,12]{1,2,0:T(8,128)S(1)}, u32[]{:S(2)}, u32[]{:S(2)}) %collective-permute-start.33) | collective-permute-done | bytes 2336 | tf_op jit(solution)/shard_map/ppermute | solution.py:51
  341.0 3.4 collective-permute-done.34
  (327 shorter events, 57.3 us)
Async XLA Ops:
  7.2 15.0 %copy-start = (bf16[2048,768]{1,0:T(8,128)(2,1)S(1)}, bf16[2048,768]{1,0:T(8,128)(2,1)}, u32[]{:S(2)}) copy-start(bf16[2048,768]{1,0:T(8,128)(2,1)} %param.29) | copy-start | bytes 9437188
  7.2 117.4 %all-gather.3.cloned.1.call-start = ((), (), s32[]{:S(2)}) async-start(), calls=%async_computation.4 | async-start | bytes 9732096 | tf_op jit(solution)/shard_map/all_gather | solution.py:424
  10.2 8.3 %collective-permute-start = (bf16[1,24,1536]{2,1,0:T(8,128)(2,1)S(1)}, bf16[1,24,1536]{2,1,0:T(8,128)(2,1)S(1)}, u32[]{:S(2)}, u32[]{:S(2)}) collective-permute-start(bf16[1,24,1536]{2,1,0:T(8,128)(2,1)S(1)} %slice_bitcast_fusion), channel_id=1, source_target_pairs={{0,4},{1,5},{2,6},{3,7},{4,0},{5,1},{6,2},{7,3},{8,12},{9,13},{10,... | collective-permute-start | bytes 221192 | tf_op jit(solution)/shard_map/ppermute | solution.py:51
  11.5 8.6 %collective-permute-start.1 = (bf16[1,24,1664]{2,1,0:T(8,128)(2,1)S(1)}, bf16[1,24,1664]{2,1,0:T(8,128)(2,1)S(1)}, u32[]{:S(2)}, u32[]{:S(2)}) collective-permute-start(bf16[1,24,1664]{2,1,0:T(8,128)(2,1)S(1)} %fusion.55), channel_id=1, source_target_pairs={{0,4},{1,5},{2,6},{3,7},{4,0},{5,1},{6,2},{7,3},{8,12},{9,13},{10,... | collective-permute-start | bytes 239624 | tf_op jit(solution)/shard_map/ppermute | solution.py:51
  14.9 42.1 %copy-start.77 = (s32[512]{0:T(512)}, s32[512]{0:T(512)S(1)}, u32[]{:S(2)}) copy-start(s32[512]{0:T(512)S(1)} %broadcast_select_fusion) | copy-start | bytes 6148
  20.1 9.7 %collective-permute-start.2 = (bf16[2,24,1536]{2,1,0:T(8,128)(2,1)S(1)}, bf16[2,24,1536]{2,1,0:T(8,128)(2,1)S(1)}, u32[]{:S(2)}, u32[]{:S(2)}) collective-permute-start(bf16[2,24,1536]{2,1,0:T(8,128)(2,1)S(1)} %pad_maximum_fusion.15), channel_id=1, source_target_pairs={{0,2},{1,3},{2,0},{3,1},{4,6},{5,7},{6,4},{7,5},{8,10},{9,11},{10,... | collective-permute-start | bytes 442376 | tf_op jit(solution)/shard_map/ppermute | solution.py:51
  20.2 15.4 %collective-permute-start.3 = (bf16[2,24,1664]{2,1,0:T(8,128)(2,1)S(1)}, bf16[2,24,1664]{2,1,0:T(8,128)(2,1)S(1)}, u32[]{:S(2)}, u32[]{:S(2)}) collective-permute-start(bf16[2,24,1664]{2,1,0:T(8,128)(2,1)S(1)} %pad_maximum_fusion.14), channel_id=1, source_target_pairs={{0,2},{1,3},{2,0},{3,1},{4,6},{5,7},{6,4},{7,5},{8,10},{9,11},{10,... | collective-permute-start | bytes 479240 | tf_op jit(solution)/shard_map/ppermute | solution.py:51
  35.7 12.2 %collective-permute-start.5 = (bf16[4,24,1664]{2,1,0:T(8,128)(2,1)S(1)}, bf16[4,24,1664]{2,1,0:T(8,128)(2,1)S(1)}, u32[]{:S(2)}, u32[]{:S(2)}) collective-permute-start(bf16[4,24,1664]{2,1,0:T(8,128)(2,1)S(1)} %pad_maximum_fusion.10), channel_id=1, source_target_pairs={{0,16},{1,17},{2,18},{3,19},{4,20},{5,21},{6,22},{7,23},{8,24},{9,... | collective-permute-start | bytes 958472 | tf_op jit(solution)/shard_map/ppermute | solution.py:51
  36.3 11.3 %collective-permute-start.4 = (bf16[4,24,1536]{2,1,0:T(8,128)(2,1)S(1)}, bf16[4,24,1536]{2,1,0:T(8,128)(2,1)S(1)}, u32[]{:S(2)}, u32[]{:S(2)}) collective-permute-start(bf16[4,24,1536]{2,1,0:T(8,128)(2,1)S(1)} %pad_maximum_fusion.11), channel_id=1, source_target_pairs={{0,1},{1,0},{2,3},{3,2},{4,5},{5,4},{6,7},{7,6},{8,9},{9,8},{10,11... | collective-permute-start | bytes 884744 | tf_op jit(solution)/shard_map/ppermute | solution.py:51
  48.1 23.6 %collective-permute-start.7 = (bf16[8,24,1664]{2,1,0:T(8,128)(2,1)S(1)}, bf16[8,24,1664]{2,1,0:T(8,128)(2,1)S(1)}, u32[]{:S(2)}, u32[]{:S(2)}) collective-permute-start(bf16[8,24,1664]{2,1,0:T(8,128)(2,1)S(1)} %pad_maximum_fusion.6), channel_id=1, source_target_pairs={{0,1},{1,0},{2,3},{3,2},{4,5},{5,4},{6,7},{7,6},{8,9},{9,8},{10,11... | collective-permute-start | bytes 1916936 | tf_op jit(solution)/shard_map/ppermute | solution.py:51
  48.5 23.2 %collective-permute-start.6 = (bf16[8,24,1536]{2,1,0:T(8,128)(2,1)S(1)}, bf16[8,24,1536]{2,1,0:T(8,128)(2,1)S(1)}, u32[]{:S(2)}, u32[]{:S(2)}) collective-permute-start(bf16[8,24,1536]{2,1,0:T(8,128)(2,1)S(1)} %pad_maximum_fusion.9), channel_id=1, source_target_pairs={{0,16},{1,17},{2,18},{3,19},{4,20},{5,21},{6,22},{7,23},{8,24},{9,... | collective-permute-start | bytes 1769480 | tf_op jit(solution)/shard_map/ppermute | solution.py:51
  50.7 28.5 %all-to-all-start.1 = ((bf16[32,16,768]{2,1,0:T(8,128)(2,1)}), bf16[32,16,768]{2,1,0:T(8,128)(2,1)S(1)}, u32[]{:S(2)}, u32[]{:S(2)}) async-start(bf16[32,16,768]{2,1,0:T(8,128)(2,1)} %bitcast.7), calls=%async_computation.1 | async-start | bytes 1572864 | tf_op jit(solution)/shard_map/all_to_all | solution.py:408
  73.0 14.7 %collective-permute-start.9 = (bf16[16,24,1536]{2,1,0:T(8,128)(2,1)}, bf16[16,24,1536]{2,1,0:T(8,128)(2,1)}, u32[]{:S(2)}, u32[]{:S(2)}) collective-permute-start(bf16[16,24,1536]{2,1,0:T(8,128)(2,1)} %pad_maximum_fusion.3), channel_id=1, source_target_pairs={{0,8},{1,9},{2,10},{3,11},{4,12},{5,13},{6,14},{7,15},{8,0},{9,1},... | collective-permute-start | bytes 3538952 | tf_op jit(solution)/shard_map/ppermute | solution.py:51
  74.2 12.9 %copy-start.80 = (s32[32]{0:T(128)}, s32[32]{0:T(128)S(1)}, u32[]{:S(2)}) copy-start(s32[32]{0:T(128)S(1)} %gather_fusion) | copy-start | bytes 388
  74.9 12.6 %copy-start.81 = (s32[32]{0:T(128)}, s32[32]{0:T(128)S(1)}, u32[]{:S(2)}) copy-start(s32[32]{0:T(128)S(1)} %gather_fusion.2) | copy-start | bytes 388
  75.1 19.6 %collective-permute-start.8 = (bf16[16,24,1664]{2,1,0:T(8,128)(2,1)S(1)}, bf16[16,24,1664]{2,1,0:T(8,128)(2,1)}, u32[]{:S(2)}, u32[]{:S(2)}) collective-permute-start(bf16[16,24,1664]{2,1,0:T(8,128)(2,1)S(1)} %pad_maximum_fusion.2), channel_id=1, source_target_pairs={{0,8},{1,9},{2,10},{3,11},{4,12},{5,13},{6,14},{7,15},{8,0},{9,1},... | collective-permute-start | bytes 3833864 | tf_op jit(solution)/shard_map/ppermute | solution.py:51
  79.2 38.7 %copy-start.10 = (bf16[32,16,768]{2,1,0:T(8,128)(2,1)}, bf16[32,16,768]{2,1,0:T(8,128)(2,1)S(1)}, u32[]{:S(2)}) copy-start(bf16[32,16,768]{2,1,0:T(8,128)(2,1)S(1)} %all-to-all-done.1) | copy-start | bytes 2359300
  79.2 42.2 %all-to-all-start = ((bf16[32,16,768]{2,1,0:T(8,128)(2,1)}), bf16[32,16,768]{2,1,0:T(8,128)(2,1)}, u32[]{:S(2)}, u32[]{:S(2)}) async-start(bf16[32,16,768]{2,1,0:T(8,128)(2,1)} %bitcast.175), calls=%async_computation | async-start | bytes 1572864 | tf_op jit(solution)/shard_map/all_to_all | solution.py:408
  87.2 15.7 %copy-start.60 = (f32[512]{0:T(512)}, f32[512]{0:T(512)S(1)}, u32[]{:S(2)}) copy-start(f32[512]{0:T(512)S(1)} %div.103) | copy-start | bytes 6148
  87.6 15.3 %copy-start.63 = (f32[512]{0:T(512)}, f32[512]{0:T(512)S(1)}, u32[]{:S(2)}) copy-start(f32[512]{0:T(512)S(1)} %rsqrt.21) | copy-start | bytes 6148
  108.0 9.9 %copy-start.3 = (bf16[512,1536]{1,0:T(8,128)(2,1)}, bf16[512,1536]{1,0:T(8,128)(2,1)S(1)}, u32[]{:S(2)}) copy-start(bf16[512,1536]{1,0:T(8,128)(2,1)S(1)} %fusion.6.q.k) | copy-start | bytes 4718596
  121.4 42.4 %copy-start.13 = (f32[512,768]{1,0:T(8,128)}, f32[512,768]{1,0:T(8,128)S(1)}, u32[]{:S(2)}) copy-start(f32[512,768]{1,0:T(8,128)S(1)} %get-tuple-element.157) | copy-start | bytes 4718596
  124.7 31.0 %copy-start.82 = (s32[32]{0:T(128)S(1)}, s32[32]{0:T(128)}, u32[]{:S(2)}) copy-start(s32[32]{0:T(128)} %constant.46.clone) | copy-start | bytes 388
  155.1 12.6 %collective-permute-start.10 = (bf16[16,96,768]{2,1,0:T(8,128)(2,1)}, bf16[16,96,768]{2,1,0:T(8,128)(2,1)}, u32[]{:S(2)}, u32[]{:S(2)}) collective-permute-start(bf16[16,96,768]{2,1,0:T(8,128)(2,1)} %get-tuple-element.136), channel_id=1, source_target_pairs={{0,8},{1,9},{2,10},{3,11},{4,12},{5,13},{6,14},{7,15},{8,0},{9,1},... | collective-permute-start | bytes 7077896 | tf_op jit(solution)/shard_map/ppermute | solution.py:51
  155.4 12.2 %collective-permute-start.11 = (bf16[16,24,3072]{2,1,0:T(8,128)(2,1)}, bf16[16,24,3072]{2,1,0:T(8,128)(2,1)}, u32[]{:S(2)}, u32[]{:S(2)}) collective-permute-start(bf16[16,24,3072]{2,1,0:T(8,128)(2,1)} %get-tuple-element.137), channel_id=1, source_target_pairs={{0,8},{1,9},{2,10},{3,11},{4,12},{5,13},{6,14},{7,15},{8,0},{9,1},... | collective-permute-start | bytes 7077896 | tf_op jit(solution)/shard_map/ppermute | solution.py:51
  155.7 41.8 %copy-start.73 = (s32[1024]{0:T(1024)}, s32[1024]{0:T(1024)S(1)}, u32[]{:S(2)}) copy-start(s32[1024]{0:T(1024)S(1)} %pad_clamp_fusion.1) | copy-start | bytes 12292
  208.1 41.6 %all-to-all-start.2 = ((bf16[32,16,768]{2,1,0:T(8,128)(2,1)}), bf16[32,16,768]{2,1,0:T(8,128)(2,1)}, u32[]{:S(2)}, u32[]{:S(2)}) async-start(bf16[32,16,768]{2,1,0:T(8,128)(2,1)} %bitcast.155), calls=%async_computation.2 | async-start | bytes 1572864 | tf_op jit(solution)/shard_map/all_to_all | solution.py:408
  214.3 35.3 %collective-permute-start.12 = (bf16[8,96,768]{2,1,0:T(8,128)(2,1)}, bf16[8,96,768]{2,1,0:T(8,128)(2,1)}, u32[]{:S(2)}, u32[]{:S(2)}) collective-permute-start(bf16[8,96,768]{2,1,0:T(8,128)(2,1)} %get-tuple-element.161), channel_id=1, source_target_pairs={{0,16},{1,17},{2,18},{3,19},{4,20},{5,21},{6,22},{7,23},{8,24},{9,... | collective-permute-start | bytes 3538952 | tf_op jit(solution)/shard_map/ppermute | solution.py:51
  214.9 34.7 %collective-permute-start.13 = (bf16[8,24,3072]{2,1,0:T(8,128)(2,1)}, bf16[8,24,3072]{2,1,0:T(8,128)(2,1)}, u32[]{:S(2)}, u32[]{:S(2)}) collective-permute-start(bf16[8,24,3072]{2,1,0:T(8,128)(2,1)} %get-tuple-element.162), channel_id=1, source_target_pairs={{0,1},{1,0},{2,3},{3,2},{4,5},{5,4},{6,7},{7,6},{8,9},{9,8},{10,11... | collective-permute-start | bytes 3538952 | tf_op jit(solution)/shard_map/ppermute | solution.py:51
  226.0 23.7 %collective-permute-start.14 = (bf16[16,24,1536]{2,1,0:T(8,128)(2,1)}, bf16[16,24,1536]{2,1,0:T(8,128)(2,1)}, u32[]{:S(2)}, u32[]{:S(2)}) collective-permute-start(bf16[16,24,1536]{2,1,0:T(8,128)(2,1)} %pad_maximum_fusion.4), channel_id=1, source_target_pairs={{0,8},{1,9},{2,10},{3,11},{4,12},{5,13},{6,14},{7,15},{8,0},{9,1},... | collective-permute-start | bytes 3538952 | tf_op jit(solution)/shard_map/ppermute | solution.py:51
  227.7 22.0 %collective-permute-start.15 = (bf16[16,24,1536]{2,1,0:T(8,128)(2,1)}, bf16[16,24,1536]{2,1,0:T(8,128)(2,1)}, u32[]{:S(2)}, u32[]{:S(2)}) collective-permute-start(bf16[16,24,1536]{2,1,0:T(8,128)(2,1)} %pad_maximum_fusion.5), channel_id=1, source_target_pairs={{0,8},{1,9},{2,10},{3,11},{4,12},{5,13},{6,14},{7,15},{8,0},{9,1},... | collective-permute-start | bytes 3538952 | tf_op jit(solution)/shard_map/ppermute | solution.py:51
  238.9 10.7 %copy-start.21 = (bf16[8,96,768]{2,1,0:T(8,128)(2,1)S(1)}, bf16[8,96,768]{2,1,0:T(8,128)(2,1)}, u32[]{:S(2)}) copy-start(bf16[8,96,768]{2,1,0:T(8,128)(2,1)} %get-tuple-element.246) | copy-start | bytes 3538948
  259.6 20.5 %collective-permute-start.16 = (bf16[4,96,768]{2,1,0:T(8,128)(2,1)}, bf16[4,96,768]{2,1,0:T(8,128)(2,1)}, u32[]{:S(2)}, u32[]{:S(2)}) collective-permute-start(bf16[4,96,768]{2,1,0:T(8,128)(2,1)} %get-tuple-element.173), channel_id=1, source_target_pairs={{0,1},{1,0},{2,3},{3,2},{4,5},{5,4},{6,7},{7,6},{8,9},{9,8},{10,11... | collective-permute-start | bytes 1769480 | tf_op jit(solution)/shard_map/ppermute | solution.py:51
  260.9 21.1 %collective-permute-start.17 = (bf16[4,24,3072]{2,1,0:T(8,128)(2,1)}, bf16[4,24,3072]{2,1,0:T(8,128)(2,1)S(1)}, u32[]{:S(2)}, u32[]{:S(2)}) collective-permute-start(bf16[4,24,3072]{2,1,0:T(8,128)(2,1)} %get-tuple-element.174), channel_id=1, source_target_pairs={{0,16},{1,17},{2,18},{3,19},{4,20},{5,21},{6,22},{7,23},{8,24},{9,... | collective-permute-start | bytes 1769480 | tf_op jit(solution)/shard_map/ppermute | solution.py:51
  261.5 34.7 %collective-permute-start.18 = (bf16[8,24,1536]{2,1,0:T(8,128)(2,1)}, bf16[8,24,1536]{2,1,0:T(8,128)(2,1)}, u32[]{:S(2)}, u32[]{:S(2)}) collective-permute-start(bf16[8,24,1536]{2,1,0:T(8,128)(2,1)} %get-tuple-element.175), channel_id=1, source_target_pairs={{0,16},{1,17},{2,18},{3,19},{4,20},{5,21},{6,22},{7,23},{8,24},{9,... | collective-permute-start | bytes 1769480 | tf_op jit(solution)/shard_map/ppermute | solution.py:51
  262.9 33.3 %collective-permute-start.19 = (bf16[8,24,1536]{2,1,0:T(8,128)(2,1)}, bf16[8,24,1536]{2,1,0:T(8,128)(2,1)}, u32[]{:S(2)}, u32[]{:S(2)}) collective-permute-start(bf16[8,24,1536]{2,1,0:T(8,128)(2,1)} %get-tuple-element.176), channel_id=1, source_target_pairs={{0,1},{1,0},{2,3},{3,2},{4,5},{5,4},{6,7},{7,6},{8,9},{9,8},{10,11... | collective-permute-start | bytes 1769480 | tf_op jit(solution)/shard_map/ppermute | solution.py:51
  263.7 6.5 %collective-permute-start.20 = (f32[16,24,12]{1,2,0:T(8,128)S(1)}, f32[16,24,12]{1,2,0:T(8,128)S(1)}, u32[]{:S(2)}, u32[]{:S(2)}) collective-permute-start(f32[16,24,12]{1,2,0:T(8,128)S(1)} %slice.356), channel_id=1, source_target_pairs={{0,8},{1,9},{2,10},{3,11},{4,12},{5,13},{6,14},{7,15},{8,0},{9,1},... | collective-permute-start | bytes 55304 | tf_op jit(solution)/shard_map/ppermute | solution.py:51
  263.8 49.4 %all-to-all-start.3 = ((bf16[32,16,768]{2,1,0:T(8,128)(2,1)}), bf16[32,16,768]{2,1,0:T(8,128)(2,1)}, u32[]{:S(2)}, u32[]{:S(2)}) async-start(bf16[32,16,768]{2,1,0:T(8,128)(2,1)} %bitcast.40), calls=%async_computation.3 | async-start | bytes 1572864 | tf_op jit(solution)/shard_map/all_to_all | solution.py:408
  282.0 14.2 %copy-start.45 = (bf16[4,24,3072]{2,1,0:T(8,128)(2,1)}, bf16[4,24,3072]{2,1,0:T(8,128)(2,1)S(1)}, u32[]{:S(2)}) copy-start(bf16[4,24,3072]{2,1,0:T(8,128)(2,1)S(1)} %collective-permute-done.17) | copy-start | bytes 1769476
  300.1 9.9 %collective-permute-start.21 = (bf16[2,96,768]{2,1,0:T(8,128)(2,1)S(1)}, bf16[2,96,768]{2,1,0:T(8,128)(2,1)S(1)}, u32[]{:S(2)}, u32[]{:S(2)}) collective-permute-start(bf16[2,96,768]{2,1,0:T(8,128)(2,1)S(1)} %get-tuple-element.186), channel_id=1, source_target_pairs={{0,2},{1,3},{2,0},{3,1},{4,6},{5,7},{6,4},{7,5},{8,10},{9,11},{10,... | collective-permute-start | bytes 884744 | tf_op jit(solution)/shard_map/ppermute | solution.py:51
  300.9 12.4 %collective-permute-start.22 = (bf16[2,24,3072]{2,1,0:T(8,128)(2,1)S(1)}, bf16[2,24,3072]{2,1,0:T(8,128)(2,1)S(1)}, u32[]{:S(2)}, u32[]{:S(2)}) collective-permute-start(bf16[2,24,3072]{2,1,0:T(8,128)(2,1)S(1)} %get-tuple-element.187), channel_id=1, source_target_pairs={{0,2},{1,3},{2,0},{3,1},{4,6},{5,7},{6,4},{7,5},{8,10},{9,11},{10,... | collective-permute-start | bytes 884744 | tf_op jit(solution)/shard_map/ppermute | solution.py:51
  302.1 11.1 %collective-permute-start.23 = (bf16[4,24,1536]{2,1,0:T(8,128)(2,1)S(1)}, bf16[4,24,1536]{2,1,0:T(8,128)(2,1)S(1)}, u32[]{:S(2)}, u32[]{:S(2)}) collective-permute-start(bf16[4,24,1536]{2,1,0:T(8,128)(2,1)S(1)} %get-tuple-element.188), channel_id=1, source_target_pairs={{0,1},{1,0},{2,3},{3,2},{4,5},{5,4},{6,7},{7,6},{8,9},{9,8},{10,11... | collective-permute-start | bytes 884744 | tf_op jit(solution)/shard_map/ppermute | solution.py:51
  302.7 10.5 %collective-permute-start.24 = (bf16[4,24,1536]{2,1,0:T(8,128)(2,1)S(1)}, bf16[4,24,1536]{2,1,0:T(8,128)(2,1)S(1)}, u32[]{:S(2)}, u32[]{:S(2)}) collective-permute-start(bf16[4,24,1536]{2,1,0:T(8,128)(2,1)S(1)} %get-tuple-element.189), channel_id=1, source_target_pairs={{0,16},{1,17},{2,18},{3,19},{4,20},{5,21},{6,22},{7,23},{8,24},{9,... | collective-permute-start | bytes 884744 | tf_op jit(solution)/shard_map/ppermute | solution.py:51
  304.1 5.6 %collective-permute-start.25 = (f32[8,24,12]{1,2,0:T(8,128)S(1)}, f32[8,24,12]{1,2,0:T(8,128)S(1)}, u32[]{:S(2)}, u32[]{:S(2)}) collective-permute-start(f32[8,24,12]{1,2,0:T(8,128)S(1)} %get-tuple-element.190), channel_id=1, source_target_pairs={{0,1},{1,0},{2,3},{3,2},{4,5},{5,4},{6,7},{7,6},{8,9},{9,8},{10,11... | collective-permute-start | bytes 27656 | tf_op jit(solution)/shard_map/ppermute | solution.py:51
  310.0 10.7 %copy-start.51 = (bf16[2,96,768]{2,1,0:T(8,128)(2,1)}, bf16[2,96,768]{2,1,0:T(8,128)(2,1)S(1)}, u32[]{:S(2)}) copy-start(bf16[2,96,768]{2,1,0:T(8,128)(2,1)S(1)} %collective-permute-done.21) | copy-start | bytes 884740
  313.5 20.0 %copy-start.41 = (f32[24,3072]{1,0:T(8,128)S(1)}, f32[24,3072]{1,0:T(8,128)}, u32[]{:S(2)}) copy-start(f32[24,3072]{1,0:T(8,128)} %param.40) | copy-start | bytes 884740
  313.5 19.9 %copy-start.47 = (f32[24,3072]{1,0:T(8,128)S(1)}, f32[24,3072]{1,0:T(8,128)}, u32[]{:S(2)}) copy-start(f32[24,3072]{1,0:T(8,128)} %param.41) | copy-start | bytes 884740
  313.5 19.9 %copy-start.48 = (f32[24,3072]{1,0:T(8,128)S(1)}, f32[24,3072]{1,0:T(8,128)}, u32[]{:S(2)}) copy-start(f32[24,3072]{1,0:T(8,128)} %param.42) | copy-start | bytes 884740
  313.5 10.2 %collective-permute-start.26 = (bf16[2,24,1536]{2,1,0:T(8,128)(2,1)S(1)}, bf16[2,24,1536]{2,1,0:T(8,128)(2,1)S(1)}, u32[]{:S(2)}, u32[]{:S(2)}) collective-permute-start(bf16[2,24,1536]{2,1,0:T(8,128)(2,1)S(1)} %get-tuple-element.198), channel_id=1, source_target_pairs={{0,2},{1,3},{2,0},{3,1},{4,6},{5,7},{6,4},{7,5},{8,10},{9,11},{10,... | collective-permute-start | bytes 442376 | tf_op jit(solution)/shard_map/ppermute | solution.py:51
  314.4 9.4 %collective-permute-start.27 = (bf16[2,24,1536]{2,1,0:T(8,128)(2,1)S(1)}, bf16[2,24,1536]{2,1,0:T(8,128)(2,1)S(1)}, u32[]{:S(2)}, u32[]{:S(2)}) collective-permute-start(bf16[2,24,1536]{2,1,0:T(8,128)(2,1)S(1)} %get-tuple-element.199), channel_id=1, source_target_pairs={{0,2},{1,3},{2,0},{3,1},{4,6},{5,7},{6,4},{7,5},{8,10},{9,11},{10,... | collective-permute-start | bytes 442376 | tf_op jit(solution)/shard_map/ppermute | solution.py:51
  315.6 8.1 %collective-permute-start.28 = (f32[4,24,12]{1,2,0:T(8,128)S(1)}, f32[4,24,12]{1,2,0:T(8,128)S(1)}, u32[]{:S(2)}, u32[]{:S(2)}) collective-permute-start(f32[4,24,12]{1,2,0:T(8,128)S(1)} %get-tuple-element.200), channel_id=1, source_target_pairs={{0,16},{1,17},{2,18},{3,19},{4,20},{5,21},{6,22},{7,23},{8,24},{9,... | collective-permute-start | bytes 13832 | tf_op jit(solution)/shard_map/ppermute | solution.py:51
  320.7 19.1 %copy-start.42 = (f32[96,768]{1,0:T(8,128)S(1)}, f32[96,768]{1,0:T(8,128)}, u32[]{:S(2)}) copy-start(f32[96,768]{1,0:T(8,128)} %param.43) | copy-start | bytes 884740
  320.7 19.1 %copy-start.49 = (f32[96,768]{1,0:T(8,128)S(1)}, f32[96,768]{1,0:T(8,128)}, u32[]{:S(2)}) copy-start(f32[96,768]{1,0:T(8,128)} %param.44) | copy-start | bytes 884740
  320.7 19.1 %copy-start.50 = (f32[96,768]{1,0:T(8,128)S(1)}, f32[96,768]{1,0:T(8,128)}, u32[]{:S(2)}) copy-start(f32[96,768]{1,0:T(8,128)} %param.45) | copy-start | bytes 884740
  320.7 12.7 %collective-permute-start.31 = (bf16[1,24,3072]{2,1,0:T(8,128)(2,1)S(1)}, bf16[1,24,3072]{2,1,0:T(8,128)(2,1)S(1)}, u32[]{:S(2)}, u32[]{:S(2)}) collective-permute-start(bf16[1,24,3072]{2,1,0:T(8,128)(2,1)S(1)} %add_convert_fusion.29), channel_id=1, source_target_pairs={{0,4},{1,5},{2,6},{3,7},{4,0},{5,1},{6,2},{7,3},{8,12},{9,13},{10,... | collective-permute-start | bytes 442376 | tf_op jit(solution)/shard_map/ppermute | solution.py:51
  321.6 18.3 %copy-start.52 = (bf16[2,96,768]{2,1,0:T(8,128)(2,1)S(1)}, bf16[2,96,768]{2,1,0:T(8,128)(2,1)}, u32[]{:S(2)}) copy-start(bf16[2,96,768]{2,1,0:T(8,128)(2,1)} %copy-done.51) | copy-start | bytes 884740
  321.6 18.2 %collective-permute-start.32 = (bf16[1,96,768]{2,1,0:T(8,128)(2,1)S(1)}, bf16[1,96,768]{2,1,0:T(8,128)(2,1)S(1)}, u32[]{:S(2)}, u32[]{:S(2)}) collective-permute-start(bf16[1,96,768]{2,1,0:T(8,128)(2,1)S(1)} %add_convert_fusion.30), channel_id=1, source_target_pairs={{0,4},{1,5},{2,6},{3,7},{4,0},{5,1},{6,2},{7,3},{8,12},{9,13},{10,... | collective-permute-start | bytes 442376 | tf_op jit(solution)/shard_map/ppermute | solution.py:51
  323.8 21.2 %collective-permute-start.30 = (bf16[1,24,1536]{2,1,0:T(8,128)(2,1)S(1)}, bf16[1,24,1536]{2,1,0:T(8,128)(2,1)S(1)}, u32[]{:S(2)}, u32[]{:S(2)}) collective-permute-start(bf16[1,24,1536]{2,1,0:T(8,128)(2,1)S(1)} %add_convert_fusion.33), channel_id=1, source_target_pairs={{0,4},{1,5},{2,6},{3,7},{4,0},{5,1},{6,2},{7,3},{8,12},{9,13},{10,... | collective-permute-start | bytes 221192 | tf_op jit(solution)/shard_map/ppermute | solution.py:51
  324.7 21.1 %collective-permute-start.29 = (bf16[1,24,1536]{2,1,0:T(8,128)(2,1)S(1)}, bf16[1,24,1536]{2,1,0:T(8,128)(2,1)S(1)}, u32[]{:S(2)}, u32[]{:S(2)}) collective-permute-start(bf16[1,24,1536]{2,1,0:T(8,128)(2,1)S(1)} %add_convert_fusion.32), channel_id=1, source_target_pairs={{0,4},{1,5},{2,6},{3,7},{4,0},{5,1},{6,2},{7,3},{8,12},{9,13},{10,... | collective-permute-start | bytes 221192 | tf_op jit(solution)/shard_map/ppermute | solution.py:51
  326.8 12.9 %collective-permute-start.33 = (f32[2,24,12]{1,2,0:T(8,128)S(1)}, f32[2,24,12]{1,2,0:T(8,128)S(1)}, u32[]{:S(2)}, u32[]{:S(2)}) collective-permute-start(f32[2,24,12]{1,2,0:T(8,128)S(1)} %get-tuple-element.208), channel_id=1, source_target_pairs={{0,2},{1,3},{2,0},{3,1},{4,6},{5,7},{6,4},{7,5},{8,10},{9,11},{10,... | collective-permute-start | bytes 6920 | tf_op jit(solution)/shard_map/ppermute | solution.py:51
  334.6 10.4 %copy-start.54 = (f32[24,768]{1,0:T(8,128)S(1)}, f32[24,768]{1,0:T(8,128)}, u32[]{:S(2)}) copy-start(f32[24,768]{1,0:T(8,128)} %param.37) | copy-start | bytes 221188
  334.6 10.4 %copy-start.57 = (f32[24,768]{1,0:T(8,128)S(1)}, f32[24,768]{1,0:T(8,128)}, u32[]{:S(2)}) copy-start(f32[24,768]{1,0:T(8,128)} %param.38) | copy-start | bytes 221188
  334.6 10.4 %copy-start.58 = (f32[24,768]{1,0:T(8,128)S(1)}, f32[24,768]{1,0:T(8,128)}, u32[]{:S(2)}) copy-start(f32[24,768]{1,0:T(8,128)} %param.39) | copy-start | bytes 221188
  339.7 4.6 %collective-permute-start.34 = (f32[1,24,12]{1,2,0:T(8,128)S(1)}, f32[1,24,12]{1,2,0:T(8,128)S(1)}, u32[]{:S(2)}, u32[]{:S(2)}) collective-permute-start(f32[1,24,12]{1,2,0:T(8,128)S(1)} %slice_add_fusion.6), channel_id=1, source_target_pairs={{0,4},{1,5},{2,6},{3,7},{4,0},{5,1},{6,2},{7,3},{8,12},{9,13},{10,... | collective-permute-start | bytes 3464 | tf_op jit(solution)/shard_map/ppermute | solution.py:51
  (60 other events, 205.2 us)
Sparse Core Ops, SparseCore 0:
  11.5 113.0 all-gather.2
where the time goes:
time: 360 us; the launch traced here: 354 us
  waiting for transfers between devices  97.5 us (27%)
  other arithmetic  59.8 us (17%)
  starting transfers between devices  55.5 us (15%)
  Pallas kernels  54.6 us (15%)
  matrix products  36.2 us (10%)
  local copies, waits for them, and re-layouts  34.7 us (10%)
  between operations  15.5 us (4%)
    ppermute x35, waiting for transfers between devices, swap(): lax.ppermute(values, AXES, [(d, d ^ 1 << bit) for d in range(devices)])  90.2 us
    dot_general x18, matrix products, dot(): lax.dot_general(left, right, (dims, ((), ())), preferred_element_type=f32)  36.2 us
    pallas_call x1, Pallas kernels, mlp(): pl.pallas_call(mlp_kernel, grid_spec=grid_spec, out_shape=[jax.ShapeDtype...  30.4 us
    ppermute x35, starting transfers between devices, swap(): lax.ppermute(values, AXES, [(d, d ^ 1 << bit) for d in range(devices)])  28.8 us
    all_to_all x4, starting transfers between devices, send(): lax.all_to_all(blocks, AXES, split_axis=0, concat_axis=0, tiled=True)  26.6 us
    pallas_call x2, Pallas kernels, attention(): pl.pallas_call(attend_kernel if extra is None else attend_back_kernel, gr...  24.1 us
    convert_element_type x12, other arithmetic, merge(): (keep[:half].astype(f32) + got[:half].astype(f32)).astype(self.kind)  21.8 us
    gather x4, local copies, waits for them, and re-layouts, by_place(): return jnp.take(blocks, ranks, axis=0, mode='clip')  8.43 us
  transfers between devices with their start and end apart: 40, of which 19 were waited for; matrix products, arithmetic and copies ran while one was open for 24% of the time, Pallas kernels for 3%

commit v1 on v0

--- a/solution.py
+++ b/solution.py
@@ -81,8 +81,8 @@
 
 
 class Chain:
-    def __init__(self, keep, send, order, kind=bf16):
-        self.keep, self.send, self.order, self.kind = keep, send, list(order), kind
+    def __init__(self, keep, send, order):
+        self.keep, self.send, self.order = keep, send, list(order)
         self.launch()
 
     def launch(self):
@@ -91,8 +91,8 @@
     def merge(self):
         half = self.keep.shape[0] // 2
         keep, got = self.keep, self.got
-        self.send = (keep[half:].astype(f32) + got[half:].astype(f32)).astype(self.kind)
-        self.keep = (keep[:half].astype(f32) + got[:half].astype(f32)).astype(self.kind)
+        self.send = keep[half:] + got[half:]
+        self.keep = keep[:half] + got[:half]
 
     def total(self):
         return (self.keep.astype(f32) + self.got.astype(f32))[0]
@@ -157,6 +157,18 @@
     return values
 
 
+def store_by_place(place, block, keep, send):
+    half = keep.shape[0]
+
+    @pl.when(place < half)
+    def _():
+        keep[place] = block
+
+    @pl.when(place >= half)
+    def _():
+        send[place - half] = block
+
+
 def mlp_kernel(
     place_r, place_e, a2, dy, we, wr, bias,
     out_y, out_da, keep_r, send_r, keep_e, send_e, out_gb, u_all, dz_all, we_all,
@@ -193,27 +205,18 @@
 
     out_gb[...] = lax.fori_loop(0, tokens // TOKEN_BLOCK, chunk, jnp.zeros(out_gb.shape, f32))
 
-    def store(place, block, keep, send):
-        @pl.when(place < half)
-        def _():
-            keep[place] = block
-
-        @pl.when(place >= half)
-        def _():
-            send[place - half] = block
-
     rows_r = keep_r.shape[1]
     per_step = HIDDEN_BLOCK // rows_r
     grad = dot(u_all[...], dy[...], ((0,), (0,))).astype(bf16)
     for j in range(per_step):
-        store(place_r[step * per_step + j], grad[j * rows_r : (j + 1) * rows_r], keep_r, send_r)
+        store_by_place(place_r[step * per_step + j], grad[j * rows_r : (j + 1) * rows_r], keep_r, send_r)
     grad = dot(a2[...], dz_all[...], ((0,), (0,))).astype(bf16)
     if len(keep_e.shape) == 2:
         keep_e[...] = grad
     else:
         rows_e = keep_e.shape[1]
         for s in range(2 * half):
-            store(place_e[s], grad[s * rows_e : (s + 1) * rows_e], keep_e, send_e)
+            store_by_place(place_e[s], grad[s * rows_e : (s + 1) * rows_e], keep_e, send_e)
 
 
 def mlp(a2, dy, both, bias, order_r, order_e):
@@ -316,7 +319,7 @@
     out_lse[...] = jnp.where(first, both_lse[0], both_lse[1])
 
 
-def attend_back_kernel(q, k, v, d_out, lse, seg_col, seg_row, out_dq, out_dk, out_dv):
+def attend_back_kernel(q, k, v, d_out, lse, seg_col, seg_row, out):
     parts = []
     for head in range(2):
         mine = head_lanes(q.shape, head)
@@ -335,8 +338,8 @@
             )
         )
     first = head_lanes(q.shape, 0)
-    for ref, left, right in zip((out_dq, out_dk, out_dv), *parts):
-        ref[...] = jnp.where(first, left, right).astype(bf16)
+    for number, (left, right) in enumerate(zip(*parts)):
+        out[number] = jnp.where(first, left, right).astype(bf16)
 
 
 def attention(query_key, values, segments, extra=None):
@@ -349,13 +352,17 @@
     seg_specs = [whole(tokens, 1), whole(1, tokens)]
     shape = lambda kind: jax.ShapeDtypeStruct((tokens, features), kind)
     more = [] if extra is None else list(extra)
-    outs = [shape(bf16), shape(f32)] if extra is None else [shape(bf16)] * 3
+    if extra is None:
+        outs, out_specs = [shape(bf16), shape(f32)], [head, head]
+    else:
+        outs = jax.ShapeDtypeStruct((3, tokens, features), bf16)
+        out_specs = pl.BlockSpec((3, tokens, 2 * HEAD_DIM), lambda i: (0, 0, i))
     products = 2 if extra is None else 5
     return pl.pallas_call(
         attend_kernel if extra is None else attend_back_kernel,
         grid=(pairs,),
         in_specs=[head, key, head] + [head] * len(more) + seg_specs,
-        out_specs=[head] * len(outs),
+        out_specs=out_specs,
         out_shape=outs,
         compiler_params=pltpu.CompilerParams(
             dimension_semantics=("arbitrary",), vmem_limit_bytes=48 << 20
@@ -367,6 +374,127 @@
         ),
         name="attend" if extra is None else "attend_back",
     )(query_key, query_key, values, *more, *segs)
+
+
+def sums_of(*parts):
+    rows = [jnp.sum(part.astype(f32), axis=0, keepdims=True) for part in parts]
+    return jnp.concatenate(rows + [jnp.zeros_like(rows[0])] * (8 - len(rows)), axis=0)
+
+
+def middle_kernel(middle, branch, d_two, dy, gain, bias, wm, y, d_middle, d_branch, d_out, sums):
+    normed, factor = normalize(middle[...])
+    y[...] = (middle[...] + branch[...] + bias[...]).astype(bf16)
+    upstream = dy[...].astype(f32)
+    grad = upstream + norm_back(d_two[...], normed, factor, gain[...])
+    low = grad.astype(bf16)
+    d_middle[...] = grad
+    d_branch[...] = low
+    d_out[...] = dot(low, wm[...], ((1,), (1,))).astype(bf16)
+
+    @pl.when(pl.program_id(0) == 0)
+    def _():
+        sums[...] = jnp.zeros_like(sums)
+
+    sums[...] += sums_of(low, d_two[...] * normed, d_two[...], upstream)
+
+
+def first_kernel(grads, w_qk, w_v, x, d_middle, gain, dx, sums):
+    features = x.shape[1]
+    d_one = dot(grads[0], w_qk[:, :features], ((1,), (1,)))
+    d_one += dot(grads[1], w_qk[:, features:], ((1,), (1,)))
+    d_one += dot(grads[2], w_v[...], ((1,), (1,)))
+    normed, factor = normalize(x[...].astype(f32))
+    dx[...] = (d_middle[...] + norm_back(d_one, normed, factor, gain[...])).astype(bf16)
+
+    @pl.when(pl.program_id(0) == 0)
+    def _():
+        sums[...] = jnp.zeros_like(sums)
+
+    sums[...] += sums_of(d_one * normed, d_one, grads[0], grads[2])
+
+
+def by_rows(kernel, tokens, operands, out_kinds, flops):
+    features = operands[0].shape[-1]
+
+    def spec(shape):
+        if len(shape) > 1 and shape[-2] == tokens:
+            lead = len(shape) - 2
+            return pl.BlockSpec(
+                shape[:-2] + (TOKEN_BLOCK, shape[-1]), lambda i: (0,) * lead + (i, 0)
+            )
+        return pl.BlockSpec(shape, lambda i: (0,) * len(shape))
+
+    outs = [jax.ShapeDtypeStruct((tokens, features), kind) for kind in out_kinds]
+    outs.append(jax.ShapeDtypeStruct((8, features), f32))
+    return pl.pallas_call(
+        kernel,
+        grid=(tokens // TOKEN_BLOCK,),
+        in_specs=[spec(x.shape) for x in operands],
+        out_specs=[spec(x.shape) for x in outs],
+        out_shape=outs,
+        compiler_params=pltpu.CompilerParams(
+            dimension_semantics=("arbitrary",), vmem_limit_bytes=48 << 20
+        ),
+        cost_estimate=pl.CostEstimate(
+            flops=flops,
+            transcendentals=0,
+            bytes_accessed=sum(x.size * x.dtype.itemsize for x in [*operands, *outs]),
+        ),
+    )(*operands)
+
+
+def products_kernel(place_qk, place_vm, a1, o, grads, dbr, keep_qk, send_qk, keep_vm, send_vm):
+    step = pl.program_id(0)
+    last = step == 3
+    left = jnp.where(last, o[...].astype(f32), a1[...].astype(f32)).astype(bf16)
+    right = jnp.where(last, dbr[...].astype(f32), grads[...].astype(f32)).astype(bf16)
+    out = dot(left, right, ((0,), (0,))).astype(bf16)
+    half, rows = keep_qk.shape[:2]
+
+    @pl.when(step < 2)
+    def _():
+        for s in range(2 * half):
+            store_by_place(place_qk[s], out[s * rows : (s + 1) * rows], keep_qk, send_qk)
+
+    @pl.when(step >= 2)
+    def _():
+        for s in range(2 * half):
+            store_by_place(place_vm[s], out[s * rows : (s + 1) * rows], keep_vm, send_vm)
+
+
+def product_chains(a1, o, grads, dbr, order_qk, order_vm):
+    devices = lax.axis_size(AXES)
+    tokens, features = a1.shape
+    rows, half = features // devices, devices // 2
+    if rows % 8:
+        return (
+            weight_chain([(a1, grads[0]), (a1, grads[1])], order_qk),
+            weight_chain([(a1, grads[2]), (o, dbr)], order_vm),
+        )
+    whole = pl.BlockSpec((tokens, features), lambda i, *_: (0, 0))
+    spec_qk = pl.BlockSpec((half, rows, features), lambda i, *_: (0, 0, jnp.minimum(i, 1)))
+    spec_vm = pl.BlockSpec((half, rows, features), lambda i, *_: (0, 0, jnp.maximum(i - 2, 0)))
+    third = pl.BlockSpec((None, tokens, features), lambda i, *_: (jnp.minimum(i, 2), 0, 0))
+    keep_qk, send_qk, keep_vm, send_vm = pl.pallas_call(
+        products_kernel,
+        grid_spec=pltpu.PrefetchScalarGridSpec(
+            num_scalar_prefetch=2,
+            grid=(4,),
+            in_specs=[whole, whole, third, whole],
+            out_specs=[spec_qk, spec_qk, spec_vm, spec_vm],
+        ),
+        out_shape=[jax.ShapeDtypeStruct((half, rows, 2 * features), bf16)] * 4,
+        compiler_params=pltpu.CompilerParams(
+            dimension_semantics=("arbitrary",), vmem_limit_bytes=48 << 20
+        ),
+        cost_estimate=pl.CostEstimate(
+            flops=8 * tokens * features * features,
+            transcendentals=0,
+            bytes_accessed=12 * tokens * features + 8 * features * features,
+        ),
+        name="products",
+    )(block_places(order_qk), block_places(order_vm), a1, o, grads, dbr)
+    return Chain(keep_qk, send_qk, order_qk), Chain(keep_vm, send_vm, order_vm)
 
 
 def on_device(
@@ -445,14 +573,14 @@
     bias_hidden = vectors[8:].reshape(-1)
 
     inputs = arrived.astype(f32)
-    normed_one, factor_one = normalize(inputs)
+    normed_one, _ = normalize(inputs)
     layer_one = (normed_one * gain_one + shift_one).astype(bf16)
     joined_bias = jnp.concatenate([bias_query, jnp.zeros_like(bias_query)])
     query_key = (dot(layer_one, early) + joined_bias).astype(bf16)
     values = (dot(layer_one, w_value) + bias_value).astype(bf16)
     attended, log_total = attention(query_key, values, segments)
     middle = inputs + dot(attended, w_mixing) + bias_mixing
-    normed_two, factor_two = normalize(middle)
+    normed_two, _ = normalize(middle)
     layer_two = (normed_two * gain_two + shift_two).astype(bf16)
     branch, d_layer_two, grad_reduce, grad_expand, grad_hidden = mlp(
         layer_two, arrived_grad, w_mlp, bias_hidden, first, second
@@ -460,44 +588,34 @@
     chain_reduce = Chain(*grad_reduce, first)
     chain_expand = Chain(*grad_expand, second)
     chains = [chain_reduce, chain_expand]
-    outputs = (middle + branch + bias_output).astype(bf16)
-
-    upstream = arrived_grad.astype(f32)
-    d_middle = upstream + norm_back(d_layer_two, normed_two, factor_two, gain_two)
-    d_branch = d_middle.astype(bf16)
-    d_attended = dot(d_branch, w_mixing, ((1,), (1,))).astype(bf16)
-    early_reads = (d_attended, outputs, layer_one, attended, d_branch, d_layer_two, normed_two, upstream)
-    early_reads = turn(early_reads, chains)
-    d_attended, outputs, layer_one, attended, d_branch, d_layer_two, normed_two, upstream = early_reads
+
+    outputs, d_middle, d_branch, d_attended, sums_two = by_rows(
+        middle_kernel,
+        holding,
+        [middle, branch, d_layer_two, arrived_grad, gain_two[None], bias_output[None], w_mixing],
+        [bf16, f32, bf16, bf16],
+        2 * holding * features * features,
+    )
+    d_attended, outputs = turn((d_attended, outputs), chains)
     moved = send(outputs)
-    d_query, d_key, d_value = attention(query_key, values, segments, (d_attended, log_total))
-    chain_late = weight_chain([(layer_one, d_value), (attended, d_branch)], first)
-    chain_query_key = weight_chain([(layer_one, d_query), (layer_one, d_key)], second)
-    chains += [chain_late, chain_query_key]
-    d_query_key = jnp.concatenate([d_query, d_key], axis=1)
-    d_layer_one = dot(d_query_key, early, ((1,), (1,))) + dot(d_value, w_value, ((1,), (1,)))
-    input_grads = d_middle + norm_back(d_layer_one, normed_one, factor_one, gain_one)
-    input_grads = input_grads.astype(bf16)
-    total = lambda part: jnp.sum(part.astype(f32), axis=0, keepdims=True)
+    grads = attention(query_key, values, segments, (d_attended, log_total))
+    chains += product_chains(layer_one, attended, grads, d_branch, second, first)
+    chain_query_key, chain_late = chains[2:]
+    input_grads, sums_one = by_rows(
+        first_kernel,
+        holding,
+        [grads, early, w_value, arrived, d_middle, gain_one[None]],
+        [bf16],
+        6 * holding * features * features,
+    )
     grad_vector = jnp.concatenate(
-        [
-            total(d_layer_one * normed_one),
-            total(d_layer_one),
-            total(d_query),
-            total(d_value),
-            total(d_branch),
-            total(d_layer_two * normed_two),
-            total(d_layer_two),
-            total(upstream),
-            grad_hidden.reshape(-1, features),
-        ],
-        axis=0,
+        [sums_one[:4], sums_two[:4], grad_hidden.reshape(-1, features)], axis=0
     )
     vector_blocks = grad_vector.T.reshape(devices, -1, lines)
     vector_blocks = by_place(vector_blocks, second)
     input_grads, vector_blocks, moved = turn((input_grads, vector_blocks, moved), chains)
     moved_grad = send(input_grads)
-    chain_vector = Chain(*halves(vector_blocks), second, f32)
+    chain_vector = Chain(*halves(vector_blocks), second)
     chains.append(chain_vector)
     moved = turn(moved, chains)
     grid_output = put_rows(moved)

time: 360 us -> 331 us (0.919)
  the two profiles are of different devices: /device:TPU:30 before, /device:TPU:0 now
where the time goes in v1:
time: 331 us; the launch traced here: 329 us
  waiting for transfers between devices  93.3 us (28%)
  Pallas kernels  72.5 us (22%)
  starting transfers between devices  59.7 us (18%)
  other arithmetic  40 us (12%)
  local copies, waits for them, and re-layouts  28.8 us (9%)
  matrix products  20.1 us (6%)
  between operations  15 us (5%)
    ppermute x35, waiting for transfers between devices, swap(): lax.ppermute(values, AXES, [(d, d ^ 1 << bit) for d in range(devices)])  74.9 us
    ppermute x35, starting transfers between devices, swap(): lax.ppermute(values, AXES, [(d, d ^ 1 << bit) for d in range(devices)])  36.3 us
    pallas_call x1, Pallas kernels, mlp(): pl.pallas_call(mlp_kernel, grid_spec=grid_spec, out_shape=[jax.ShapeDtype...  29.9 us
    pallas_call x2, Pallas kernels, attention(): pl.pallas_call(attend_kernel if extra is None else attend_back_kernel, gr...  23.7 us
    all_to_all x4, starting transfers between devices, send(): lax.all_to_all(blocks, AXES, split_axis=0, concat_axis=0, tiled=True)  23.4 us
    dot_general x7, matrix products, dot(): lax.dot_general(left, right, (dims, ((), ())), preferred_element_type=f32)  20.1 us
    all_to_all x4, waiting for transfers between devices, send(): lax.all_to_all(blocks, AXES, split_axis=0, concat_axis=0, tiled=True)  17.6 us
    add x14, other arithmetic, merge(): self.keep = keep[:half] + got[:half]  17.1 us
  transfers between devices with their start and end apart: 40, of which 18 were waited for; matrix products, arithmetic and copies ran while one was open for 18% of the time, Pallas kernels for 13%

profile of v1, /device:TPU:0, one launch (start us, length us, event | category | flops | bytes accessed | tf_op | source)
XLA Modules:
  0.0 329.5 jit_solution(3667428704930785709)
XLA Ops:
  10.2 4.1 %collective-permute-start = (bf16[1,24,1536]{2,1,0:T(8,128)(2,1)S(1)}, bf16[1,24,1536]{2,1,0:T(8,128)(2,1)S(1)}, u32[]{:S(2)}, u32[]{:S(2)}) collective-permute-start(bf16[1,24,1536]{2,1,0:T(8,128)(2,1)S(1)} %slice_bitcast_fusion), channel_id=1, source_target_pairs={{0,4},{1,5},{2,6},{3,7},{4,0},{5,1},{6,2},{7,3},{8,12},{9,13},{10,... | collective-permute-start | bytes 221192 | tf_op jit(solution)/shard_map/ppermute | solution.py:51
  16.1 2.1 collective-permute-done
  18.3 3.6 %collective-permute-done.1 = bf16[1,24,1664]{2,1,0:T(8,128)(2,1)S(1)} collective-permute-done((bf16[1,24,1664]{2,1,0:T(8,128)(2,1)S(1)}, bf16[1,24,1664]{2,1,0:T(8,128)(2,1)S(1)}, u32[]{:S(2)}, u32[]{:S(2)}) %collective-permute-start.1) | collective-permute-done | bytes 79904 | tf_op jit(solution)/shard_map/ppermute | solution.py:51
  22.5 1.6 collective-permute-start.3
  24.0 2.8 fusion.22
  26.9 3.6 %collective-permute-done.2 = bf16[2,24,1536]{2,1,0:T(8,128)(2,1)S(1)} collective-permute-done((bf16[2,24,1536]{2,1,0:T(8,128)(2,1)S(1)}, bf16[2,24,1536]{2,1,0:T(8,128)(2,1)S(1)}, u32[]{:S(2)}, u32[]{:S(2)}) %collective-permute-start.2) | collective-permute-done | bytes 147488 | tf_op jit(solution)/shard_map/ppermute | solution.py:51
  30.4 4.8 %collective-permute-done.3 = bf16[2,24,1664]{2,1,0:T(8,128)(2,1)S(1)} collective-permute-done((bf16[2,24,1664]{2,1,0:T(8,128)(2,1)S(1)}, bf16[2,24,1664]{2,1,0:T(8,128)(2,1)S(1)}, u32[]{:S(2)}, u32[]{:S(2)}) %collective-permute-start.3) | collective-permute-done | bytes 159776 | tf_op jit(solution)/shard_map/ppermute | solution.py:51
  35.3 1.5 collective-permute-start.5
  36.8 1.5 collective-permute-start.4
  38.3 6.2 %collective-permute-done.4 = bf16[4,24,1536]{2,1,0:T(8,128)(2,1)S(1)} collective-permute-done((bf16[4,24,1536]{2,1,0:T(8,128)(2,1)S(1)}, bf16[4,24,1536]{2,1,0:T(8,128)(2,1)S(1)}, u32[]{:S(2)}, u32[]{:S(2)}) %collective-permute-start.4) | collective-permute-done | bytes 294944 | tf_op jit(solution)/shard_map/ppermute | solution.py:51
  44.7 1.6 collective-permute-start.7
  46.7 11.9 %all-to-all-start = ((bf16[32,16,768]{2,1,0:T(8,128)(2,1)}), bf16[32,16,768]{2,1,0:T(8,128)(2,1)S(1)}, u32[]{:S(2)}, u32[]{:S(2)}) async-start(bf16[32,16,768]{2,1,0:T(8,128)(2,1)} %bitcast.5), calls=%async_computation | async-start | bytes 1572864 | tf_op jit(solution)/shard_map/all_to_all | solution.py:536
  58.6 4.8 %fusion.23 = bf16[512,768]{1,0:T(8,128)(2,1)} fusion(bf16[2048,768]{1,0:T(8,128)(2,1)} %param.28, s32[512]{0:T(512)S(1)} %broadcast_select_fusion), kind=kOutput, calls=%fused_computation.39 | convolution fusion | flops 1612054528 | bytes 3934208 | tf_op jit(solution)/shard_map/dot_general | solution.py:46
  63.4 4.0 %collective-permute-done.6 = bf16[8,24,1536]{2,1,0:T(8,128)(2,1)S(1)} collective-permute-done((bf16[8,24,1536]{2,1,0:T(8,128)(2,1)S(1)}, bf16[8,24,1536]{2,1,0:T(8,128)(2,1)S(1)}, u32[]{:S(2)}, u32[]{:S(2)}) %collective-permute-start.6) | collective-permute-done | bytes 589856 | tf_op jit(solution)/shard_map/ppermute | solution.py:51
  68.5 1.2 pad_maximum_fusion.2
  71.8 12.8 %all-to-all-done = bf16[32,16,768]{2,1,0:T(8,128)(2,1)S(1)} async-done(((bf16[32,16,768]{2,1,0:T(8,128)(2,1)}), bf16[32,16,768]{2,1,0:T(8,128)(2,1)S(1)}, u32[]{:S(2)}, u32[]{:S(2)}) %all-to-all-start) | async-done | bytes 786464 | tf_op jit(solution)/shard_map/all_to_all | solution.py:536
  84.6 2.8 all-to-all-start.1
  88.2 3.3 pad_maximum_fusion.1
  91.4 3.9 %gather_fusion.3 = bf16[32,24,1536]{2,1,0:T(8,128)(2,1)} fusion(bf16[32,24,1536]{2,1,0:T(8,128)(2,1)} %pad_maximum_fusion.1, s32[1024]{0:T(1024)S(1)} %pad_clamp_fusion.1), kind=kCustom, calls=%fused_computation.3 | custom fusion | bytes 4718720 | tf_op jit(solution)/shard_map/jit(_take)/gather | solution.py:145
  95.3 3.5 %pad_maximum_fusion = bf16[32,24,1664]{2,1,0:T(8,128)(2,1)} fusion(bf16[16,24,1664]{2,1,0:T(8,128)(2,1)} %collective-permute-done.8, bf16[16,24,1664]{2,1,0:T(8,128)(2,1)} %pad_maximum_fusion.2), kind=kLoop, calls=%fused_computation.14 | loop fusion | flops 1277952 | bytes 5111808 | tf_op jit(solution)/shard_map/concatenate | solution.py:141
  98.8 4.0 %gather_fusion.1 = bf16[32,24,1664]{2,1,0:T(8,128)(2,1)} fusion(bf16[32,24,1664]{2,1,0:T(8,128)(2,1)} %pad_maximum_fusion, s32[1024]{0:T(1024)S(1)} %pad_clamp_fusion.2), kind=kCustom, calls=%fused_computation.1 | custom fusion | bytes 5111936 | tf_op jit(solution)/shard_map/jit(_take)/gather | solution.py:145
  104.7 1.3 copy-done.34
  107.7 1.4 fusion.6.q.k
  109.8 9.2 %attend.1 = (bf16[512,768]{1,0:T(8,128)(2,1)S(1)}, f32[512,768]{1,0:T(8,128)S(1)}) custom-call(bf16[512,1536]{1,0:T(8,128)(2,1)S(1)} %fusion.6.q.k, bf16[512,1536]{1,0:T(8,128)(2,1)S(1)} %fusion.6.q.k, bf16[512,768]{1,0:T(8,128)(2,1)S(1)} %add_convert_fusion.1.v, s32[512,1]{1,0:T(8,128)S(1)} %copy.51.seg_col, s32[1,512]{1,0:T(1,128)S(1)} %copy-done.14), custom_call_target="tpu_custom_call" | custom-call | flops 1610612736 | bytes 6291456 | tf_op jit(solution)/shard_map/attend/pallas_call | solution.py:361
  121.6 1.2 add_convert_fusion.a2
  122.8 4.8 %all-to-all-done.1 = bf16[32,16,768]{2,1,0:T(8,128)(2,1)S(1)} async-done(((bf16[32,16,768]{2,1,0:T(8,128)(2,1)}), bf16[32,16,768]{2,1,0:T(8,128)(2,1)S(1)}, u32[]{:S(2)}, u32[]{:S(2)}) %all-to-all-start.1) | async-done | bytes 786464 | tf_op jit(solution)/shard_map/all_to_all | solution.py:536
  128.5 29.9 %mlp.1 = (f32[512,768]{1,0:T(8,128)}, f32[512,768]{1,0:T(8,128)}, bf16[16,96,768]{2,1,0:T(8,128)(2,1)}, bf16[16,96,768]{2,1,0:T(8,128)(2,1)}, bf16[16,24,3072]{2...) custom-call(s32[32]{0:T(128)} %copy-done.15, s32[32]{0:T(128)} %copy-done.17, ...), custom_call_target="tpu_custom_call" | custom-call | flops 14495514624 | bytes 23592960 | tf_op jit(solution)/shard_map/mlp/pallas_call | solution.py:268
  159.8 4.4 %shard_map.386 = (bf16[512,768]{1,0:T(8,128)(2,1)S(1)}, f32[512,768]{1,0:T(8,128)S(1)}, bf16[512,768]{1,0:T(8,128)(2,1)S(1)}, bf16[512,768]{1,0:T(8,128)(2,1)S(1)}, f32[8,768]{1,0:T(8,128)S(1)}) custom-call(f32[512,768]{1,0:T(8,128)} %copy-done.33, f32[512,768]{1,0:T(8,128)} %get-tuple-element.130.branch, f32[512,768]{1,0:T(8,128)} %get-tuple-element.131.d_two, ...), custom_call_target="tpu_custom_call" | custom-call | flops 603979776 | bytes 10647552 | tf_op jit(solution)/shard_map/pallas_call | solution.py:429
  164.2 2.4 collective-permute-done.11
  166.6 1.4 copy-done.41
  168.0 3.4 %slice_add_fusion.1 = (bf16[8,96,768]{2,1,0:T(8,128)(2,1)}, bf16[8,96,768]{2,1,0:T(8,128)(2,1)}) fusion(bf16[16,96,768]{2,1,0:T(8,128)(2,1)} %collective-permute-done.10, bf16[16,96,768]{2,1,0:T(8,128)(2,1)S(1)} %copy-done.40), kind=kLoop, calls=%fused_computation.43 | loop fusion | flops 1179648 | bytes 7077888 | tf_op jit(solution)/shard_map/add | solution.py:95
  171.5 1.6 slice_add_fusion
  173.1 3.6 %all-to-all-start.2 = ((bf16[32,16,768]{2,1,0:T(8,128)(2,1)}), bf16[32,16,768]{2,1,0:T(8,128)(2,1)}, u32[]{:S(2)}, u32[]{:S(2)}) async-start(bf16[32,16,768]{2,1,0:T(8,128)(2,1)} %bitcast.82), calls=%async_computation.2 | async-start | bytes 1572864 | tf_op jit(solution)/shard_map/all_to_all | solution.py:536
  177.6 1.1 copy-done.22
  178.8 1.4 copy-done.26
  180.2 1.4 copy-done.28
  181.6 1.1 copy-done.30
  182.7 14.6 %attend_back.1.grads = bf16[3,512,768]{2,1,0:T(8,128)(2,1)} custom-call(bf16[512,1536]{1,0:T(8,128)(2,1)S(1)} %copy-done.26, bf16[512,1536]{1,0:T(8,128)(2,1)S(1)} %copy-done.26, bf16[512,768]{1,0:T(8,128)(2,1)S(1)} %copy-done.30, bf16[512,768]{1,0:T(8,128)(2,1)S(1)} %copy-done.22, f32[512,768]{1,0:T(8,128)S(1)} %copy-done.28, s32[512,1]{1,0:T(8,128)S(1)} %copy-done.12, ...), custom_call_target="tpu_custom_call" | custom-call | flops 4026531840 | bytes 6291456 | tf_op jit(solution)/shard_map/attend_back/pallas_call | solution.py:361
  197.3 8.7 %products.1 = (bf16[16,24,1536]{2,1,0:T(8,128)(2,1)S(1)}, bf16[16,24,1536]{2,1,0:T(8,128)(2,1)}, bf16[16,24,1536]{2,1,0:T(8,128)(2,1)S(1)}, bf16[16,24,1536]{2,1,0:T(8,128)(2,1)}) custom-call(s32[32]{0:T(128)S(1)} %copy-done.18, s32[32]{0:T(128)S(1)} %copy-done.16, bf16[512,768]{1,0:T(8,128)(2,1)S(1)} %copy-done.10, bf16[512,768]{1,0:T(8,128)(2,1)S(1)} %copy-done.24, ...), custom_call_target="tpu_custom_call" | custom-call | flops 2415919104 | bytes 9437184 | tf_op jit(solution)/shard_map/products/pallas_call | solution.py:478
  208.6 1.7 collective-permute-start.12
  210.4 1.5 collective-permute-start.13
  212.9 1.4 reduce.19
  215.7 5.8 %shard_map.387 = (bf16[512,768]{1,0:T(8,128)(2,1)}, f32[8,768]{1,0:T(8,128)S(1)}) custom-call(bf16[3,512,768]{2,1,0:T(8,128)(2,1)} %attend_back.1.grads, bf16[768,1536]{1,0:T(8,128)(2,1)} %bitcast.88, bf16[768,768]{1,0:T(8,128)(2,1)S(1)} %get-tuple-element.227.w_v, bf16[512,768]{1,0:T(8,128)(2,1)S(1)} %bitcast.79, ...), custom_call_target="tpu_custom_call" | custom-call | flops 1811939328 | bytes 9071616 | tf_op jit(solution)/shard_map/pallas_call | solution.py:429
  222.6 14.4 %collective-permute-done.12 = bf16[8,96,768]{2,1,0:T(8,128)(2,1)} collective-permute-done((bf16[8,96,768]{2,1,0:T(8,128)(2,1)}, bf16[8,96,768]{2,1,0:T(8,128)(2,1)}, u32[]{:S(2)}, u32[]{:S(2)}) %collective-permute-start.12) | collective-permute-done | bytes 1179680 | tf_op jit(solution)/shard_map/ppermute | solution.py:51
  237.0 1.4 collective-permute-done.13
  238.4 2.3 slice_add_fusion.5
  240.8 2.4 slice_add_fusion.4
  243.2 2.8 slice_add_fusion.8
  245.9 1.5 collective-permute-start.16
  248.3 1.6 collective-permute-start.19
  250.0 5.1 %all-to-all-start.3 = ((bf16[32,16,768]{2,1,0:T(8,128)(2,1)}), bf16[32,16,768]{2,1,0:T(8,128)(2,1)}, u32[]{:S(2)}, u32[]{:S(2)}) async-start(bf16[32,16,768]{2,1,0:T(8,128)(2,1)} %bitcast.22), calls=%async_computation.3 | async-start | bytes 1572864 | tf_op jit(solution)/shard_map/all_to_all | solution.py:536
  255.2 12.7 %collective-permute-done.16 = bf16[4,96,768]{2,1,0:T(8,128)(2,1)} collective-permute-done((bf16[4,96,768]{2,1,0:T(8,128)(2,1)}, bf16[4,96,768]{2,1,0:T(8,128)(2,1)}, u32[]{:S(2)}, u32[]{:S(2)}) %collective-permute-start.16) | collective-permute-done | bytes 589856 | tf_op jit(solution)/shard_map/ppermute | solution.py:51
  267.9 12.6 %collective-permute-done.18 = bf16[8,24,1536]{2,1,0:T(8,128)(2,1)} collective-permute-done((bf16[8,24,1536]{2,1,0:T(8,128)(2,1)}, bf16[8,24,1536]{2,1,0:T(8,128)(2,1)}, u32[]{:S(2)}, u32[]{:S(2)}) %collective-permute-start.18) | collective-permute-done | bytes 589856 | tf_op jit(solution)/shard_map/ppermute | solution.py:51
  280.5 1.2 collective-permute-done.19
  286.8 1.5 collective-permute-start.21
  289.4 1.5 collective-permute-start.24
  290.8 4.7 %fusion.4 = bf16[2048,768]{1,0:T(8,128)(2,1)} fusion(bf16[512,768]{1,0:T(8,128)(2,1)} %bitcast.21, s32[512]{0:T(512)S(1)} %copy-done.65), kind=kOutput, calls=%fused_computation.10 | convolution fusion | flops 1613234176 | bytes 3934208 | tf_op jit(solution)/shard_map/dot_general | solution.py:46
  295.6 3.8 %collective-permute-done.22 = bf16[2,24,3072]{2,1,0:T(8,128)(2,1)S(1)} collective-permute-done((bf16[2,24,3072]{2,1,0:T(8,128)(2,1)S(1)}, bf16[2,24,3072]{2,1,0:T(8,128)(2,1)S(1)}, u32[]{:S(2)}, u32[]{:S(2)}) %collective-permute-start.22) | collective-permute-done | bytes 294944 | tf_op jit(solution)/shard_map/ppermute | solution.py:51
  300.0 1.5 collective-permute-start.26
  302.0 2.4 collective-permute-start.31
  305.0 4.7 %fusion.5 = bf16[2048,768]{1,0:T(8,128)(2,1)} fusion(bf16[512,768]{1,0:T(8,128)(2,1)} %bitcast.23, s32[512]{0:T(512)S(1)} %copy-done.65), kind=kOutput, calls=%fused_computation.11 | convolution fusion | flops 1613234176 | bytes 3934208 | tf_op jit(solution)/shard_map/dot_general | solution.py:46
  309.7 1.3 collective-permute-done.27
  311.3 2.7 collective-permute-start.29
  315.5 2.7 collective-permute-start.34
  (255 shorter events, 41.1 us)
Async XLA Ops:
  7.2 16.8 %copy-start = (bf16[2048,768]{1,0:T(8,128)(2,1)S(1)}, bf16[2048,768]{1,0:T(8,128)(2,1)}, u32[]{:S(2)}) copy-start(bf16[2048,768]{1,0:T(8,128)(2,1)} %param.27) | copy-start | bytes 9437188
  7.2 8.9 %copy-start.63 = (s32[1,512]{1,0:T(1,128)S(1)}, s32[1,512]{1,0:T(1,128)}, u32[]{:S(2)}) copy-start(s32[1,512]{1,0:T(1,128)} %param.29) | copy-start | bytes 6148
  7.2 121.2 %all-gather.3.cloned.1.call-start = ((), (), s32[]{:S(2)}) async-start(), calls=%async_computation.4 | async-start | bytes 9732096 | tf_op jit(solution)/shard_map/all_gather | solution.py:552
  10.2 8.0 %collective-permute-start = (bf16[1,24,1536]{2,1,0:T(8,128)(2,1)S(1)}, bf16[1,24,1536]{2,1,0:T(8,128)(2,1)S(1)}, u32[]{:S(2)}, u32[]{:S(2)}) collective-permute-start(bf16[1,24,1536]{2,1,0:T(8,128)(2,1)S(1)} %slice_bitcast_fusion), channel_id=1, source_target_pairs={{0,4},{1,5},{2,6},{3,7},{4,0},{5,1},{6,2},{7,3},{8,12},{9,13},{10,... | collective-permute-start | bytes 221192 | tf_op jit(solution)/shard_map/ppermute | solution.py:51
  15.2 6.7 %collective-permute-start.1 = (bf16[1,24,1664]{2,1,0:T(8,128)(2,1)S(1)}, bf16[1,24,1664]{2,1,0:T(8,128)(2,1)S(1)}, u32[]{:S(2)}, u32[]{:S(2)}) collective-permute-start(bf16[1,24,1664]{2,1,0:T(8,128)(2,1)S(1)} %fusion.31), channel_id=1, source_target_pairs={{0,4},{1,5},{2,6},{3,7},{4,0},{5,1},{6,2},{7,3},{8,12},{9,13},{10,... | collective-permute-start | bytes 239624 | tf_op jit(solution)/shard_map/ppermute | solution.py:51
  16.1 42.4 %copy-start.64 = (s32[512]{0:T(512)}, s32[512]{0:T(512)S(1)}, u32[]{:S(2)}) copy-start(s32[512]{0:T(512)S(1)} %broadcast_select_fusion) | copy-start | bytes 6148
  21.9 8.5 %collective-permute-start.2 = (bf16[2,24,1536]{2,1,0:T(8,128)(2,1)S(1)}, bf16[2,24,1536]{2,1,0:T(8,128)(2,1)S(1)}, u32[]{:S(2)}, u32[]{:S(2)}) collective-permute-start(bf16[2,24,1536]{2,1,0:T(8,128)(2,1)S(1)} %pad_maximum_fusion.11), channel_id=1, source_target_pairs={{0,2},{1,3},{2,0},{3,1},{4,6},{5,7},{6,4},{7,5},{8,10},{9,11},{10,... | collective-permute-start | bytes 442376 | tf_op jit(solution)/shard_map/ppermute | solution.py:51
  22.5 12.8 %collective-permute-start.3 = (bf16[2,24,1664]{2,1,0:T(8,128)(2,1)S(1)}, bf16[2,24,1664]{2,1,0:T(8,128)(2,1)S(1)}, u32[]{:S(2)}, u32[]{:S(2)}) collective-permute-start(bf16[2,24,1664]{2,1,0:T(8,128)(2,1)S(1)} %pad_maximum_fusion.10), channel_id=1, source_target_pairs={{0,2},{1,3},{2,0},{3,1},{4,6},{5,7},{6,4},{7,5},{8,10},{9,11},{10,... | collective-permute-start | bytes 479240 | tf_op jit(solution)/shard_map/ppermute | solution.py:51
  35.3 9.2 %collective-permute-start.5 = (bf16[4,24,1664]{2,1,0:T(8,128)(2,1)S(1)}, bf16[4,24,1664]{2,1,0:T(8,128)(2,1)S(1)}, u32[]{:S(2)}, u32[]{:S(2)}) collective-permute-start(bf16[4,24,1664]{2,1,0:T(8,128)(2,1)S(1)} %pad_maximum_fusion.6), channel_id=1, source_target_pairs={{0,16},{1,17},{2,18},{3,19},{4,20},{5,21},{6,22},{7,23},{8,24},{9,... | collective-permute-start | bytes 958472 | tf_op jit(solution)/shard_map/ppermute | solution.py:51
  36.8 7.7 %collective-permute-start.4 = (bf16[4,24,1536]{2,1,0:T(8,128)(2,1)S(1)}, bf16[4,24,1536]{2,1,0:T(8,128)(2,1)S(1)}, u32[]{:S(2)}, u32[]{:S(2)}) collective-permute-start(bf16[4,24,1536]{2,1,0:T(8,128)(2,1)S(1)} %pad_maximum_fusion.7), channel_id=1, source_target_pairs={{0,1},{1,0},{2,3},{3,2},{4,5},{5,4},{6,7},{7,6},{8,9},{9,8},{10,11... | collective-permute-start | bytes 884744 | tf_op jit(solution)/shard_map/ppermute | solution.py:51
  44.7 22.7 %collective-permute-start.7 = (bf16[8,24,1664]{2,1,0:T(8,128)(2,1)S(1)}, bf16[8,24,1664]{2,1,0:T(8,128)(2,1)S(1)}, u32[]{:S(2)}, u32[]{:S(2)}) collective-permute-start(bf16[8,24,1664]{2,1,0:T(8,128)(2,1)S(1)} %pad_maximum_fusion.4), channel_id=1, source_target_pairs={{0,1},{1,0},{2,3},{3,2},{4,5},{5,4},{6,7},{7,6},{8,9},{9,8},{10,11... | collective-permute-start | bytes 1916936 | tf_op jit(solution)/shard_map/ppermute | solution.py:51
  46.3 21.1 %collective-permute-start.6 = (bf16[8,24,1536]{2,1,0:T(8,128)(2,1)S(1)}, bf16[8,24,1536]{2,1,0:T(8,128)(2,1)S(1)}, u32[]{:S(2)}, u32[]{:S(2)}) collective-permute-start(bf16[8,24,1536]{2,1,0:T(8,128)(2,1)S(1)} %pad_maximum_fusion.5), channel_id=1, source_target_pairs={{0,16},{1,17},{2,18},{3,19},{4,20},{5,21},{6,22},{7,23},{8,24},{9,... | collective-permute-start | bytes 1769480 | tf_op jit(solution)/shard_map/ppermute | solution.py:51
  46.7 38.0 %all-to-all-start = ((bf16[32,16,768]{2,1,0:T(8,128)(2,1)}), bf16[32,16,768]{2,1,0:T(8,128)(2,1)S(1)}, u32[]{:S(2)}, u32[]{:S(2)}) async-start(bf16[32,16,768]{2,1,0:T(8,128)(2,1)} %bitcast.5), calls=%async_computation | async-start | bytes 1572864 | tf_op jit(solution)/shard_map/all_to_all | solution.py:536
  69.6 18.5 %collective-permute-start.9 = (bf16[16,24,1536]{2,1,0:T(8,128)(2,1)}, bf16[16,24,1536]{2,1,0:T(8,128)(2,1)}, u32[]{:S(2)}, u32[]{:S(2)}) collective-permute-start(bf16[16,24,1536]{2,1,0:T(8,128)(2,1)} %pad_maximum_fusion.3), channel_id=1, source_target_pairs={{0,8},{1,9},{2,10},{3,11},{4,12},{5,13},{6,14},{7,15},{8,0},{9,1},... | collective-permute-start | bytes 3538952 | tf_op jit(solution)/shard_map/ppermute | solution.py:51
  70.4 17.3 %copy-start.15 = (s32[32]{0:T(128)}, s32[32]{0:T(128)S(1)}, u32[]{:S(2)}) copy-start(s32[32]{0:T(128)S(1)} %gather_fusion.2) | copy-start | bytes 388
  71.1 17.0 %copy-start.17 = (s32[32]{0:T(128)}, s32[32]{0:T(128)S(1)}, u32[]{:S(2)}) copy-start(s32[32]{0:T(128)S(1)} %gather_fusion) | copy-start | bytes 388
  71.3 38.5 %copy-start.11 = (s32[512,1]{1,0:T(8,128)}, s32[512,1]{1,0:T(8,128)S(1)}, u32[]{:S(2)}) copy-start(s32[512,1]{1,0:T(8,128)S(1)} %copy.51.seg_col) | copy-start | bytes 6148
  71.3 24.0 %collective-permute-start.8 = (bf16[16,24,1664]{2,1,0:T(8,128)(2,1)}, bf16[16,24,1664]{2,1,0:T(8,128)(2,1)}, u32[]{:S(2)}, u32[]{:S(2)}) collective-permute-start(bf16[16,24,1664]{2,1,0:T(8,128)(2,1)} %pad_maximum_fusion.2), channel_id=1, source_target_pairs={{0,8},{1,9},{2,10},{3,11},{4,12},{5,13},{6,14},{7,15},{8,0},{9,1},... | collective-permute-start | bytes 3833864 | tf_op jit(solution)/shard_map/ppermute | solution.py:51
  84.6 43.0 %all-to-all-start.1 = ((bf16[32,16,768]{2,1,0:T(8,128)(2,1)}), bf16[32,16,768]{2,1,0:T(8,128)(2,1)S(1)}, u32[]{:S(2)}, u32[]{:S(2)}) async-start(bf16[32,16,768]{2,1,0:T(8,128)(2,1)} %bitcast.13), calls=%async_computation.1 | async-start | bytes 1572864 | tf_op jit(solution)/shard_map/all_to_all | solution.py:536
  109.1 9.9 %copy-start.25 = (bf16[512,1536]{1,0:T(8,128)(2,1)}, bf16[512,1536]{1,0:T(8,128)(2,1)S(1)}, u32[]{:S(2)}) copy-start(bf16[512,1536]{1,0:T(8,128)(2,1)S(1)} %fusion.6.q.k) | copy-start | bytes 4718596
  128.5 30.5 %copy-start.35 = (bf16[32,24,1664]{2,1,0:T(8,128)(2,1)S(1)}, bf16[32,24,1664]{2,1,0:T(8,128)(2,1)}, u32[]{:S(2)}) copy-start(bf16[32,24,1664]{2,1,0:T(8,128)(2,1)} %gather_fusion.1) | copy-start | bytes 7667716
  158.4 5.8 %collective-permute-start.10 = (bf16[16,96,768]{2,1,0:T(8,128)(2,1)}, bf16[16,96,768]{2,1,0:T(8,128)(2,1)}, u32[]{:S(2)}, u32[]{:S(2)}) collective-permute-start(bf16[16,96,768]{2,1,0:T(8,128)(2,1)} %get-tuple-element.134), channel_id=1, source_target_pairs={{0,8},{1,9},{2,10},{3,11},{4,12},{5,13},{6,14},{7,15},{8,0},{9,1},... | collective-permute-start | bytes 7077896 | tf_op jit(solution)/shard_map/ppermute | solution.py:51
  158.7 8.0 %collective-permute-start.11 = (bf16[16,24,3072]{2,1,0:T(8,128)(2,1)}, bf16[16,24,3072]{2,1,0:T(8,128)(2,1)S(1)}, u32[]{:S(2)}, u32[]{:S(2)}) collective-permute-start(bf16[16,24,3072]{2,1,0:T(8,128)(2,1)} %get-tuple-element.135), channel_id=1, source_target_pairs={{0,8},{1,9},{2,10},{3,11},{4,12},{5,13},{6,14},{7,15},{8,0},{9,1},... | collective-permute-start | bytes 7077896 | tf_op jit(solution)/shard_map/ppermute | solution.py:51
  164.2 8.9 %copy-start.8 = (bf16[512,768]{1,0:T(8,128)(2,1)}, bf16[512,768]{1,0:T(8,128)(2,1)S(1)}, u32[]{:S(2)}) copy-start(bf16[512,768]{1,0:T(8,128)(2,1)S(1)} %get-tuple-element.149) | copy-start | bytes 2359300
  164.2 8.9 %copy-start.13 = (f32[8,768]{1,0:T(8,128)}, f32[8,768]{1,0:T(8,128)S(1)}, u32[]{:S(2)}) copy-start(f32[8,768]{1,0:T(8,128)S(1)} %get-tuple-element.147) | copy-start | bytes 73732
  173.1 65.3 %all-to-all-start.2 = ((bf16[32,16,768]{2,1,0:T(8,128)(2,1)}), bf16[32,16,768]{2,1,0:T(8,128)(2,1)}, u32[]{:S(2)}, u32[]{:S(2)}) async-start(bf16[32,16,768]{2,1,0:T(8,128)(2,1)} %bitcast.82), calls=%async_computation.2 | async-start | bytes 1572864 | tf_op jit(solution)/shard_map/all_to_all | solution.py:536
  182.7 14.6 %copy-start.10 = (bf16[512,768]{1,0:T(8,128)(2,1)S(1)}, bf16[512,768]{1,0:T(8,128)(2,1)}, u32[]{:S(2)}) copy-start(bf16[512,768]{1,0:T(8,128)(2,1)} %copy-done.9) | copy-start | bytes 2359300
  182.7 14.6 %copy-start.16 = (s32[32]{0:T(128)S(1)}, s32[32]{0:T(128)}, u32[]{:S(2)}) copy-start(s32[32]{0:T(128)} %copy-done.15) | copy-start | bytes 388
  182.7 14.6 %copy-start.18 = (s32[32]{0:T(128)S(1)}, s32[32]{0:T(128)}, u32[]{:S(2)}) copy-start(s32[32]{0:T(128)} %copy-done.17) | copy-start | bytes 388
  182.7 14.6 %copy-start.20 = (bf16[512,768]{1,0:T(8,128)(2,1)S(1)}, bf16[512,768]{1,0:T(8,128)(2,1)}, u32[]{:S(2)}) copy-start(bf16[512,768]{1,0:T(8,128)(2,1)} %copy-done.19) | copy-start | bytes 2359300
  182.7 14.6 %copy-start.24 = (bf16[512,768]{1,0:T(8,128)(2,1)S(1)}, bf16[512,768]{1,0:T(8,128)(2,1)}, u32[]{:S(2)}) copy-start(bf16[512,768]{1,0:T(8,128)(2,1)} %copy-done.23) | copy-start | bytes 2359300
  197.3 14.5 %copy-start.66 = (s32[32]{0:T(128)S(1)}, s32[32]{0:T(128)}, u32[]{:S(2)}) copy-start(s32[32]{0:T(128)} %constant.43.clone) | copy-start | bytes 388
  208.1 14.5 %collective-permute-start.14 = (bf16[16,24,1536]{2,1,0:T(8,128)(2,1)}, bf16[16,24,1536]{2,1,0:T(8,128)(2,1)}, u32[]{:S(2)}, u32[]{:S(2)}) collective-permute-start(bf16[16,24,1536]{2,1,0:T(8,128)(2,1)} %get-tuple-element.153), channel_id=1, source_target_pairs={{0,8},{1,9},{2,10},{3,11},{4,12},{5,13},{6,14},{7,15},{8,0},{9,1},... | collective-permute-start | bytes 3538952 | tf_op jit(solution)/shard_map/ppermute | solution.py:51
  208.3 14.3 %collective-permute-start.15 = (bf16[16,24,1536]{2,1,0:T(8,128)(2,1)}, bf16[16,24,1536]{2,1,0:T(8,128)(2,1)}, u32[]{:S(2)}, u32[]{:S(2)}) collective-permute-start(bf16[16,24,1536]{2,1,0:T(8,128)(2,1)} %get-tuple-element.154), channel_id=1, source_target_pairs={{0,8},{1,9},{2,10},{3,11},{4,12},{5,13},{6,14},{7,15},{8,0},{9,1},... | collective-permute-start | bytes 3538952 | tf_op jit(solution)/shard_map/ppermute | solution.py:51
  208.6 28.4 %collective-permute-start.12 = (bf16[8,96,768]{2,1,0:T(8,128)(2,1)}, bf16[8,96,768]{2,1,0:T(8,128)(2,1)}, u32[]{:S(2)}, u32[]{:S(2)}) collective-permute-start(bf16[8,96,768]{2,1,0:T(8,128)(2,1)} %get-tuple-element.150), channel_id=1, source_target_pairs={{0,16},{1,17},{2,18},{3,19},{4,20},{5,21},{6,22},{7,23},{8,24},{9,... | collective-permute-start | bytes 3538952 | tf_op jit(solution)/shard_map/ppermute | solution.py:51
  210.4 28.0 %collective-permute-start.13 = (bf16[8,24,3072]{2,1,0:T(8,128)(2,1)}, bf16[8,24,3072]{2,1,0:T(8,128)(2,1)}, u32[]{:S(2)}, u32[]{:S(2)}) collective-permute-start(bf16[8,24,3072]{2,1,0:T(8,128)(2,1)} %get-tuple-element.151), channel_id=1, source_target_pairs={{0,1},{1,0},{2,3},{3,2},{4,5},{5,4},{6,7},{7,6},{8,9},{9,8},{10,11... | collective-permute-start | bytes 3538952 | tf_op jit(solution)/shard_map/ppermute | solution.py:51
  221.5 16.9 %copy-start.38 = (bf16[8,96,768]{2,1,0:T(8,128)(2,1)S(1)}, bf16[8,96,768]{2,1,0:T(8,128)(2,1)}, u32[]{:S(2)}) copy-start(bf16[8,96,768]{2,1,0:T(8,128)(2,1)} %get-tuple-element.225) | copy-start | bytes 3538948
  245.9 22.0 %collective-permute-start.16 = (bf16[4,96,768]{2,1,0:T(8,128)(2,1)}, bf16[4,96,768]{2,1,0:T(8,128)(2,1)}, u32[]{:S(2)}, u32[]{:S(2)}) collective-permute-start(bf16[4,96,768]{2,1,0:T(8,128)(2,1)} %get-tuple-element.165), channel_id=1, source_target_pairs={{0,1},{1,0},{2,3},{3,2},{4,5},{5,4},{6,7},{7,6},{8,9},{9,8},{10,11... | collective-permute-start | bytes 1769480 | tf_op jit(solution)/shard_map/ppermute | solution.py:51
  247.4 20.5 %collective-permute-start.17 = (bf16[4,24,3072]{2,1,0:T(8,128)(2,1)}, bf16[4,24,3072]{2,1,0:T(8,128)(2,1)}, u32[]{:S(2)}, u32[]{:S(2)}) collective-permute-start(bf16[4,24,3072]{2,1,0:T(8,128)(2,1)} %get-tuple-element.166), channel_id=1, source_target_pairs={{0,16},{1,17},{2,18},{3,19},{4,20},{5,21},{6,22},{7,23},{8,24},{9,... | collective-permute-start | bytes 1769480 | tf_op jit(solution)/shard_map/ppermute | solution.py:51
  247.9 32.5 %collective-permute-start.18 = (bf16[8,24,1536]{2,1,0:T(8,128)(2,1)}, bf16[8,24,1536]{2,1,0:T(8,128)(2,1)}, u32[]{:S(2)}, u32[]{:S(2)}) collective-permute-start(bf16[8,24,1536]{2,1,0:T(8,128)(2,1)} %get-tuple-element.167), channel_id=1, source_target_pairs={{0,1},{1,0},{2,3},{3,2},{4,5},{5,4},{6,7},{7,6},{8,9},{9,8},{10,11... | collective-permute-start | bytes 1769480 | tf_op jit(solution)/shard_map/ppermute | solution.py:51
  248.3 33.3 %collective-permute-start.19 = (bf16[8,24,1536]{2,1,0:T(8,128)(2,1)S(1)}, bf16[8,24,1536]{2,1,0:T(8,128)(2,1)}, u32[]{:S(2)}, u32[]{:S(2)}) collective-permute-start(bf16[8,24,1536]{2,1,0:T(8,128)(2,1)S(1)} %get-tuple-element.168), channel_id=1, source_target_pairs={{0,16},{1,17},{2,18},{3,19},{4,20},{5,21},{6,22},{7,23},{8,24},{9,... | collective-permute-start | bytes 1769480 | tf_op jit(solution)/shard_map/ppermute | solution.py:51
  250.0 5.2 %collective-permute-start.20 = (f32[16,24,12]{1,2,0:T(8,128)S(1)}, f32[16,24,12]{1,2,0:T(8,128)S(1)}, u32[]{:S(2)}, u32[]{:S(2)}) collective-permute-start(f32[16,24,12]{1,2,0:T(8,128)S(1)} %slice.332), channel_id=1, source_target_pairs={{0,8},{1,9},{2,10},{3,11},{4,12},{5,13},{6,14},{7,15},{8,0},{9,1},... | collective-permute-start | bytes 55304 | tf_op jit(solution)/shard_map/ppermute | solution.py:51
  250.0 49.3 %all-to-all-start.3 = ((bf16[32,16,768]{2,1,0:T(8,128)(2,1)}), bf16[32,16,768]{2,1,0:T(8,128)(2,1)}, u32[]{:S(2)}, u32[]{:S(2)}) async-start(bf16[32,16,768]{2,1,0:T(8,128)(2,1)} %bitcast.22), calls=%async_computation.3 | async-start | bytes 1572864 | tf_op jit(solution)/shard_map/all_to_all | solution.py:536
  286.1 9.4 %collective-permute-start.25 = (f32[8,24,12]{1,2,0:T(8,128)S(1)}, f32[8,24,12]{1,2,0:T(8,128)S(1)}, u32[]{:S(2)}, u32[]{:S(2)}) collective-permute-start(f32[8,24,12]{1,2,0:T(8,128)S(1)} %get-tuple-element.182), channel_id=1, source_target_pairs={{0,1},{1,0},{2,3},{3,2},{4,5},{5,4},{6,7},{7,6},{8,9},{9,8},{10,11... | collective-permute-start | bytes 27656 | tf_op jit(solution)/shard_map/ppermute | solution.py:51
  286.8 8.8 %collective-permute-start.21 = (bf16[2,96,768]{2,1,0:T(8,128)(2,1)S(1)}, bf16[2,96,768]{2,1,0:T(8,128)(2,1)S(1)}, u32[]{:S(2)}, u32[]{:S(2)}) collective-permute-start(bf16[2,96,768]{2,1,0:T(8,128)(2,1)S(1)} %get-tuple-element.178), channel_id=1, source_target_pairs={{0,2},{1,3},{2,0},{3,1},{4,6},{5,7},{6,4},{7,5},{8,10},{9,11},{10,... | collective-permute-start | bytes 884744 | tf_op jit(solution)/shard_map/ppermute | solution.py:51
  288.2 11.1 %collective-permute-start.22 = (bf16[2,24,3072]{2,1,0:T(8,128)(2,1)S(1)}, bf16[2,24,3072]{2,1,0:T(8,128)(2,1)S(1)}, u32[]{:S(2)}, u32[]{:S(2)}) collective-permute-start(bf16[2,24,3072]{2,1,0:T(8,128)(2,1)S(1)} %get-tuple-element.179), channel_id=1, source_target_pairs={{0,2},{1,3},{2,0},{3,1},{4,6},{5,7},{6,4},{7,5},{8,10},{9,11},{10,... | collective-permute-start | bytes 884744 | tf_op jit(solution)/shard_map/ppermute | solution.py:51
  288.8 10.6 %collective-permute-start.23 = (bf16[4,24,1536]{2,1,0:T(8,128)(2,1)S(1)}, bf16[4,24,1536]{2,1,0:T(8,128)(2,1)S(1)}, u32[]{:S(2)}, u32[]{:S(2)}) collective-permute-start(bf16[4,24,1536]{2,1,0:T(8,128)(2,1)S(1)} %get-tuple-element.180), channel_id=1, source_target_pairs={{0,16},{1,17},{2,18},{3,19},{4,20},{5,21},{6,22},{7,23},{8,24},{9,... | collective-permute-start | bytes 884744 | tf_op jit(solution)/shard_map/ppermute | solution.py:51
  289.4 10.0 %collective-permute-start.24 = (bf16[4,24,1536]{2,1,0:T(8,128)(2,1)S(1)}, bf16[4,24,1536]{2,1,0:T(8,128)(2,1)S(1)}, u32[]{:S(2)}, u32[]{:S(2)}) collective-permute-start(bf16[4,24,1536]{2,1,0:T(8,128)(2,1)S(1)} %get-tuple-element.181), channel_id=1, source_target_pairs={{0,1},{1,0},{2,3},{3,2},{4,5},{5,4},{6,7},{7,6},{8,9},{9,8},{10,11... | collective-permute-start | bytes 884744 | tf_op jit(solution)/shard_map/ppermute | solution.py:51
  299.5 14.7 %copy-start.43 = (f32[24,3072]{1,0:T(8,128)S(1)}, f32[24,3072]{1,0:T(8,128)}, u32[]{:S(2)}) copy-start(f32[24,3072]{1,0:T(8,128)} %param.38) | copy-start | bytes 884740
  299.5 14.7 %copy-start.47 = (f32[24,3072]{1,0:T(8,128)S(1)}, f32[24,3072]{1,0:T(8,128)}, u32[]{:S(2)}) copy-start(f32[24,3072]{1,0:T(8,128)} %param.39) | copy-start | bytes 884740
  299.5 14.7 %copy-start.48 = (f32[24,3072]{1,0:T(8,128)S(1)}, f32[24,3072]{1,0:T(8,128)}, u32[]{:S(2)}) copy-start(f32[24,3072]{1,0:T(8,128)} %param.40) | copy-start | bytes 884740
  299.6 10.1 %collective-permute-start.28 = (f32[4,24,12]{1,2,0:T(8,128)S(1)}, f32[4,24,12]{1,2,0:T(8,128)S(1)}, u32[]{:S(2)}, u32[]{:S(2)}) collective-permute-start(f32[4,24,12]{1,2,0:T(8,128)S(1)} %get-tuple-element.192), channel_id=1, source_target_pairs={{0,16},{1,17},{2,18},{3,19},{4,20},{5,21},{6,22},{7,23},{8,24},{9,... | collective-permute-start | bytes 13832 | tf_op jit(solution)/shard_map/ppermute | solution.py:51
  300.0 9.7 %collective-permute-start.26 = (bf16[2,24,1536]{2,1,0:T(8,128)(2,1)S(1)}, bf16[2,24,1536]{2,1,0:T(8,128)(2,1)S(1)}, u32[]{:S(2)}, u32[]{:S(2)}) collective-permute-start(bf16[2,24,1536]{2,1,0:T(8,128)(2,1)S(1)} %get-tuple-element.190), channel_id=1, source_target_pairs={{0,2},{1,3},{2,0},{3,1},{4,6},{5,7},{6,4},{7,5},{8,10},{9,11},{10,... | collective-permute-start | bytes 442376 | tf_op jit(solution)/shard_map/ppermute | solution.py:51
  301.5 9.5 %collective-permute-start.27 = (bf16[2,24,1536]{2,1,0:T(8,128)(2,1)S(1)}, bf16[2,24,1536]{2,1,0:T(8,128)(2,1)S(1)}, u32[]{:S(2)}, u32[]{:S(2)}) collective-permute-start(bf16[2,24,1536]{2,1,0:T(8,128)(2,1)S(1)} %get-tuple-element.191), channel_id=1, source_target_pairs={{0,2},{1,3},{2,0},{3,1},{4,6},{5,7},{6,4},{7,5},{8,10},{9,11},{10,... | collective-permute-start | bytes 442376 | tf_op jit(solution)/shard_map/ppermute | solution.py:51
  302.0 12.2 %collective-permute-start.31 = (bf16[1,24,3072]{2,1,0:T(8,128)(2,1)S(1)}, bf16[1,24,3072]{2,1,0:T(8,128)(2,1)S(1)}, u32[]{:S(2)}, u32[]{:S(2)}) collective-permute-start(bf16[1,24,3072]{2,1,0:T(8,128)(2,1)S(1)} %slice_add_fusion.26), channel_id=1, source_target_pairs={{0,4},{1,5},{2,6},{3,7},{4,0},{5,1},{6,2},{7,3},{8,12},{9,13},{10,... | collective-permute-start | bytes 442376 | tf_op jit(solution)/shard_map/ppermute | solution.py:51
  304.4 13.8 %collective-permute-start.32 = (bf16[1,96,768]{2,1,0:T(8,128)(2,1)S(1)}, bf16[1,96,768]{2,1,0:T(8,128)(2,1)S(1)}, u32[]{:S(2)}, u32[]{:S(2)}) collective-permute-start(bf16[1,96,768]{2,1,0:T(8,128)(2,1)S(1)} %slice_add_fusion.27), channel_id=1, source_target_pairs={{0,4},{1,5},{2,6},{3,7},{4,0},{5,1},{6,2},{7,3},{8,12},{9,13},{10,... | collective-permute-start | bytes 442376 | tf_op jit(solution)/shard_map/ppermute | solution.py:51
  309.7 8.5 %copy-start.44 = (f32[96,768]{1,0:T(8,128)S(1)}, f32[96,768]{1,0:T(8,128)}, u32[]{:S(2)}) copy-start(f32[96,768]{1,0:T(8,128)} %param.41) | copy-start | bytes 884740
  309.7 8.5 %copy-start.49 = (f32[96,768]{1,0:T(8,128)S(1)}, f32[96,768]{1,0:T(8,128)}, u32[]{:S(2)}) copy-start(f32[96,768]{1,0:T(8,128)} %param.42) | copy-start | bytes 884740
  309.7 8.5 %copy-start.50 = (f32[96,768]{1,0:T(8,128)S(1)}, f32[96,768]{1,0:T(8,128)}, u32[]{:S(2)}) copy-start(f32[96,768]{1,0:T(8,128)} %param.43) | copy-start | bytes 884740
  309.7 8.5 %copy-start.52 = (bf16[2,96,768]{2,1,0:T(8,128)(2,1)S(1)}, bf16[2,96,768]{2,1,0:T(8,128)(2,1)}, u32[]{:S(2)}) copy-start(bf16[2,96,768]{2,1,0:T(8,128)(2,1)} %copy-done.51) | copy-start | bytes 884740
  311.0 4.4 %collective-permute-start.33 = (f32[2,24,12]{1,2,0:T(8,128)S(1)}, f32[2,24,12]{1,2,0:T(8,128)S(1)}, u32[]{:S(2)}, u32[]{:S(2)}) collective-permute-start(f32[2,24,12]{1,2,0:T(8,128)S(1)} %get-tuple-element.200), channel_id=1, source_target_pairs={{0,2},{1,3},{2,0},{3,1},{4,6},{5,7},{6,4},{7,5},{8,10},{9,11},{10,... | collective-permute-start | bytes 6920 | tf_op jit(solution)/shard_map/ppermute | solution.py:51
  311.3 10.3 %collective-permute-start.29 = (bf16[1,24,1536]{2,1,0:T(8,128)(2,1)S(1)}, bf16[1,24,1536]{2,1,0:T(8,128)(2,1)S(1)}, u32[]{:S(2)}, u32[]{:S(2)}) collective-permute-start(bf16[1,24,1536]{2,1,0:T(8,128)(2,1)S(1)} %slice_add_fusion.30), channel_id=1, source_target_pairs={{0,4},{1,5},{2,6},{3,7},{4,0},{5,1},{6,2},{7,3},{8,12},{9,13},{10,... | collective-permute-start | bytes 221192 | tf_op jit(solution)/shard_map/ppermute | solution.py:51
  314.0 6.8 %collective-permute-start.30 = (bf16[1,24,1536]{2,1,0:T(8,128)(2,1)S(1)}, bf16[1,24,1536]{2,1,0:T(8,128)(2,1)S(1)}, u32[]{:S(2)}, u32[]{:S(2)}) collective-permute-start(bf16[1,24,1536]{2,1,0:T(8,128)(2,1)S(1)} %slice_add_fusion.29), channel_id=1, source_target_pairs={{0,4},{1,5},{2,6},{3,7},{4,0},{5,1},{6,2},{7,3},{8,12},{9,13},{10,... | collective-permute-start | bytes 221192 | tf_op jit(solution)/shard_map/ppermute | solution.py:51
  315.5 4.7 %collective-permute-start.34 = (f32[1,24,12]{1,2,0:T(8,128)S(1)}, f32[1,24,12]{1,2,0:T(8,128)S(1)}, u32[]{:S(2)}, u32[]{:S(2)}) collective-permute-start(f32[1,24,12]{1,2,0:T(8,128)S(1)} %slice_add_fusion.38), channel_id=1, source_target_pairs={{0,4},{1,5},{2,6},{3,7},{4,0},{5,1},{6,2},{7,3},{8,12},{9,13},{10,... | collective-permute-start | bytes 3464 | tf_op jit(solution)/shard_map/ppermute | solution.py:51
  (43 other events, 148.1 us)
Sparse Core Ops, SparseCore 0:
  11.5 116.8 all-gather.2
